TPU v7x, 256 devices: a whole 4x4x8 slice. The times are simulated.
256 devices in a mesh: dp: 32 (over x, z), expert: 8 (over y, core).
Axes of the slice: x: 4, y: 4, z: 8, core: 2. Of those that a mesh axis runs over, the one named last changes fastest.
Arguments:
- tokens: bfloat16 [32768, 2048], P(('dp', 'expert')), may hold values from -6 to 6
- expert_ids: int32 [32768, 8], P(('dp', 'expert')), may hold values from 0 to 127, all different within a row
- route_probs: float32 [32768, 8], P(('dp', 'expert')), may hold values from 0.05 to 1
- shard_limit: int32 [256, 128], P(('dp', 'expert')), may hold values from 4 to 8
- gate_proj: bfloat16 [256, 2048, 384], P(('dp', 'expert')), may hold values from -0.125 to 0.125
- up_proj: bfloat16 [256, 2048, 384], P(('dp', 'expert')), may hold values from -0.125 to 0.125
- down_proj: bfloat16 [256, 384, 2048], P(('dp', 'expert')), may hold values from -0.21875 to 0.21875
Outputs:
- mixed_out: bfloat16 [32768, 2048], P(('dp', 'expert'))
Inputs may be any that keep to these rules, and one draw needn't show every extreme that they name: `expert_ids`: each row names 8 different experts.
All inputs are finite; a program needn't handle non-finite values.
Results may differ from a plain program's by a relative error of at most 0.0095.
Values may be sent and summed in bfloat16 or wider, within the bound.
A program may use at most 64 MiB of HBM per device.

v0:
```python
import jax
import jax.numpy as jnp
from jax import lax
from jax.experimental import pallas as pl
from jax.experimental.pallas import tpu as pltpu
from jax.sharding import PartitionSpec as P

MESH = pl.DeviceIdType.MESH
BF = jnp.bfloat16
F32 = jnp.float32

NX, NY, NZ = 4, 4, 8
TOK = 128
SLOTS = 8
COL_CAP = 128
WIDTH = 2048
HALF = WIDTH // 2
HIDDEN = 768
PEERS = NX * NY
ROWS = PEERS * 2 * SLOTS
UNIT = 2 * SLOTS
EXPERTS = 128


def kernel(
    tokens, ids, probs, limit, gate, up, down, out,
    tok, meta, totals, gw, uw, dw, sbuf, rbuf, hid, obuf, ybuf, mix, part, own, rs_in, rs_out,
    in_sem, w_loc, w_send, w_recv, meta_send, meta_recv, tot_send, tot_recv,
    ag_send, ag_recv, d_send, d_recv, r_send, r_recv, rs_send, rs_recv,
):
    d = lax.axis_index("dp")
    c = lax.axis_index("expert")
    x, z = d // NZ, d % NZ
    y, core = c // 2, c % 2
    me = x * NY + y
    partner = (d, y * 2 + (1 - core))

    def z_peer(step):
        return (x * NZ + (z + step) % NZ, c)

    def xy_peer(i):
        px, py = (x + i % NX) % NX, (y + i // NX) % NY
        return px * NY + py, (px * NZ + z, py * 2 + core)

    def x_peer(i):
        return (((x + i) % NX) * NZ + z, c)

    def rows_of(chip):
        return pl.ds(pl.multiple_of(chip * UNIT, UNIT), UNIT)

    def remote(src, dst, send, recv, device):
        return pltpu.make_async_remote_copy(
            src_ref=src, dst_ref=dst, send_sem=send, recv_sem=recv,
            device_id=device, device_id_type=MESH,
        )

    for h in range(2):
        pltpu.make_async_copy(tokens.at[:, pl.ds(h * HALF, HALF)], tok.at[z, h], in_sem.at[h]).start()
    wide = pl.ds(pl.multiple_of(core * (HIDDEN // 2), HIDDEN // 2), HIDDEN // 2)
    weights = (
        (gate.at[0], gw.at[:, wide]), (up.at[0], uw.at[:, wide]), (down.at[0], dw.at[wide, :]),
    )
    for i, (src, dst) in enumerate(weights):
        pltpu.make_async_copy(src, dst, w_loc.at[i]).start()

    barrier = pltpu.get_barrier_semaphore()
    pl.semaphore_signal(barrier, inc=1, device_id=partner, device_id_type=MESH)

    def greet_z(i, carry):
        pl.semaphore_signal(barrier, inc=1, device_id=z_peer(i), device_id_type=MESH)
        return carry

    def greet_xy(i, carry):
        pl.semaphore_signal(barrier, inc=1, device_id=xy_peer(i)[1], device_id_type=MESH)
        return carry

    lax.fori_loop(1, NZ, greet_z, 0)
    lax.fori_loop(1, PEERS, greet_xy, 0)

    lane = lax.broadcasted_iota(jnp.int32, (TOK, EXPERTS), 1)
    row = lax.broadcasted_iota(jnp.int32, (TOK, EXPERTS), 0)
    chosen = jnp.zeros((TOK, EXPERTS), F32)
    weight = jnp.zeros((TOK, EXPERTS), F32)
    for k in range(8):
        hit = ids[:, k : k + 1] == lane
        chosen = jnp.where(hit, 1.0, chosen)
        weight = jnp.where(hit, probs[:, k : k + 1], weight)
    earlier = jnp.where(lane < row, 1.0, 0.0).astype(BF)
    rank = jnp.dot(earlier, chosen.astype(BF), preferred_element_type=F32)
    rank = jnp.where((chosen > 0.5) & (rank < limit[...].astype(F32)), rank, 1000.0)
    row_f = row.astype(F32)
    for r in range(SLOTS):
        at = rank == float(r)
        meta[z, r : r + 1, :] = jnp.sum(jnp.where(at, row_f + 1000.0, 0.0), axis=0, keepdims=True) - 1000.0
        meta[z, SLOTS + r : SLOTS + r + 1, :] = jnp.sum(jnp.where(at, weight, 0.0), axis=0, keepdims=True)

    pl.semaphore_wait(barrier, NZ - 1 + PEERS - 1 + 1)

    def ag(way, hop, h):
        block = (z + NZ - hop + 1) % NZ if way == 0 else (z + hop - 1) % NZ
        return remote(
            tok.at[block, h], tok.at[block, h], ag_send.at[way, hop - 1, h], ag_recv.at[way, hop - 1, h],
            z_peer(1 if way == 0 else NZ - 1),
        )

    def ag_arrival(way, hop, h):
        block = (z + NZ - hop) % NZ if way == 0 else (z + hop) % NZ
        return remote(
            tok.at[block, h], tok.at[block, h], ag_send.at[way, hop - 1, h], ag_recv.at[way, hop - 1, h],
            z_peer(1 if way == 0 else NZ - 1),
        )

    for h in range(2):
        pltpu.make_async_copy(tokens.at[:, pl.ds(h * HALF, HALF)], tok.at[z, h], in_sem.at[h]).wait()
        for way in range(2):
            ag(way, 1, h).start()

    def send_meta(i, carry):
        remote(meta.at[z], meta.at[z], meta_send, meta_recv, z_peer(i)).start()
        return carry

    lax.fori_loop(1, NZ, send_meta, 0)
    for i, (src, dst) in enumerate(weights):
        remote(src, dst, w_send.at[i], w_recv.at[i], partner).start()

    several = meta.at[pl.ds(0, NZ - 1)]
    remote(several, several, meta_send, meta_recv, z_peer(1)).wait_recv()

    total = jnp.zeros((1, EXPERTS), F32)
    for s in range(NZ):
        total = total + jnp.sum(jnp.where(meta[s, 0:SLOTS, :] >= 0.0, 1.0, 0.0), axis=0, keepdims=True)
    totals[x] = jnp.broadcast_to(total, (8, EXPERTS))

    def send_total(i, carry):
        remote(totals.at[x], totals.at[x], tot_send, tot_recv, x_peer(i)).start()
        return carry

    lax.fori_loop(1, NX, send_total, 0)

    def pair(g):
        return (z + NZ - g - 1) % NZ, (z + (g + 1) % 4) % NZ

    def slot_values(first, second):
        stacked = jnp.concatenate([first, second] * PEERS, axis=0)
        s = lax.broadcasted_iota(jnp.int32, (ROWS, EXPERTS), 0)
        e = lax.broadcasted_iota(jnp.int32, (ROWS, EXPERTS), 1)
        chip = s >> 4
        expert = (chip >> 2) * (NZ * NY) + z * NY + (chip & 3)
        return jnp.sum(jnp.where(e == expert, stacked, 0.0), axis=1, keepdims=True)

    def selection(g):
        a, b = pair(g)
        source = slot_values(meta[a, 0:SLOTS, :], meta[b, 0:SLOTS, :])
        s = lax.broadcasted_iota(jnp.int32, (ROWS, 2 * TOK), 0)
        t = lax.broadcasted_iota(jnp.int32, (ROWS, 2 * TOK), 1)
        second = (s >> 3) & 1
        return (t - second * TOK).astype(F32) == source

    def exchange(src, dst, send, recv, g, h):
        def one(i, carry):
            chip, device = xy_peer(i)
            remote(src.at[g, h, rows_of(chip)], dst.at[g, h, rows_of(me)], send.at[g, h], recv.at[g, h], device).start()
            return carry

        lax.fori_loop(1, PEERS, one, 0)

    def exchanged(src, dst, send, recv, g, h):
        most = pl.ds(0, (PEERS - 1) * UNIT)
        return remote(src.at[g, h, most], dst.at[g, h, most], send.at[g, h], recv.at[g, h], x_peer(1))

    def dispatch(g):
        a, b = pair(g)
        pick = jnp.where(selection(g), 1.0, 0.0).astype(BF)
        for h in range(2):
            for way in range(2):
                def arrive(way=way, h=h):
                    ag_arrival(way, g + 1, h).wait_recv()

                def forward(way=way, h=h):
                    ag(way, g + 2, h).start()

                if way == h:
                    arrive()
                    pl.when(g < 3)(forward)
                else:
                    pl.when(g < 3)(arrive)
                    pl.when(g < 2)(forward)
            for n in range(0, HALF, 512):
                both = jnp.concatenate([tok[a, h, :, n : n + 512], tok[b, h, :, n : n + 512]], axis=0)
                sbuf[g, h, :, n : n + 512] = jnp.dot(pick, both, preferred_element_type=F32).astype(BF)
            exchange(sbuf, rbuf, d_send, d_recv, g, h)
            rbuf[g, h, rows_of(me), :] = sbuf[g, h, rows_of(me), :]

    def feed_forward(g):
        for h in range(2):
            exchanged(sbuf, rbuf, d_send, d_recv, g, h).wait_recv()
        for n in range(0, HIDDEN, 256):
            cols = slice(n, n + 256)
            gv = jnp.dot(rbuf[g, 0], gw[0:HALF, cols], preferred_element_type=F32)
            gv = gv + jnp.dot(rbuf[g, 1], gw[HALF:WIDTH, cols], preferred_element_type=F32)
            uv = jnp.dot(rbuf[g, 0], uw[0:HALF, cols], preferred_element_type=F32)
            uv = uv + jnp.dot(rbuf[g, 1], uw[HALF:WIDTH, cols], preferred_element_type=F32)
            hid[:, cols] = (gv / (1.0 + jnp.exp(-gv)) * uv).astype(BF)
        for h in range(2):
            for n in range(0, HALF, 256):
                obuf[g, h, :, n : n + 256] = jnp.dot(
                    hid[...], dw[:, h * HALF + n : h * HALF + n + 256], preferred_element_type=F32
                ).astype(BF)
            ybuf[g, h, rows_of(me), :] = obuf[g, h, rows_of(me), :]

    for i, (src, dst) in enumerate(weights):
        pltpu.make_async_copy(src, dst, w_loc.at[i]).wait()
    other = pl.ds(pl.multiple_of((1 - core) * (HIDDEN // 2), HIDDEN // 2), HIDDEN // 2)
    theirs = (gw.at[:, other], uw.at[:, other], dw.at[other, :])

    def step(g, carry):
        pl.when(g < 4)(lambda: dispatch(g))

        @pl.when(g == 1)
        def _():
            for i, (src, _) in enumerate(weights):
                remote(src, theirs[i], w_send.at[i], w_recv.at[i], partner).wait_recv()

        pl.when(g > 0)(lambda: feed_forward(g - 1))
        return carry

    lax.fori_loop(0, 5, step, 0)

    for h in range(2):
        exchange(obuf, ybuf, r_send, r_recv, 3, h)

    some = totals.at[pl.ds(0, NX - 1)]
    remote(some, some, tot_send, tot_recv, x_peer(1)).wait_recv()
    before_x = jnp.zeros((1, EXPERTS), F32)
    for s in range(NX):
        before_x = before_x + jnp.where(s < x, 1.0, 0.0) * totals[s, 0:1, :]

    def kept_weight(shard):
        offset = before_x
        for s in range(NZ):
            count = jnp.sum(jnp.where(meta[s, 0:SLOTS, :] >= 0.0, 1.0, 0.0), axis=0, keepdims=True)
            offset = offset + jnp.where(s < shard, 1.0, 0.0) * count
        r = lax.broadcasted_iota(jnp.int32, (SLOTS, EXPERTS), 0).astype(F32)
        return jnp.where(offset + r < float(COL_CAP), meta[shard, SLOTS : 2 * SLOTS, :], 0.0)

    def mixing(g):
        a, b = pair(g)
        w = slot_values(kept_weight(a), kept_weight(b))
        mix[g] = jnp.where(selection(g), w, 0.0).T.astype(BF)

    def mix_step(g, carry):
        mixing(g)
        return carry

    lax.fori_loop(0, 4, mix_step, 0)

    def rs(way, g, h):
        return remote(
            rs_out.at[way, g, h], rs_in.at[way, g, h], rs_send.at[way, g, h], rs_recv.at[way, g, h],
            z_peer(1 if way == 0 else NZ - 1),
        )

    def collect(i, carry):
        g = 3 - i

        @pl.when(g > 0)
        def _():
            for h in range(2):
                exchange(obuf, ybuf, r_send, r_recv, g - 1, h)

        for h in range(2):
            exchanged(obuf, ybuf, r_send, r_recv, g, h).wait_recv()
            for n in range(0, HALF, 512):
                part[:, n : n + 512] = jnp.dot(mix[g], ybuf[g, h, :, n : n + 512], preferred_element_type=F32)

            @pl.when(g == 3)
            def _():
                own[h] = part[TOK : 2 * TOK, :]
                rs_out[h, 3, h] = part[0:TOK, :].astype(BF)
                rs(h, 3, h).start()

            @pl.when(g < 3)
            def _():
                for way in range(2):
                    mine = slice(TOK, 2 * TOK) if way == 0 else slice(0, TOK)

                    def add(way=way, mine=mine):
                        rs(way, g + 1, h).wait_recv()
                        rs_out[way, g, h] = (part[mine, :] + rs_in[way, g + 1, h].astype(F32)).astype(BF)

                    def first(way=way, mine=mine):
                        rs_out[way, g, h] = part[mine, :].astype(BF)

                    if way == h:
                        add()
                    else:
                        pl.when(g < 2)(add)
                        pl.when(g == 2)(first)
                    rs(way, g, h).start()

        return carry

    lax.fori_loop(0, 4, collect, 0)

    for h in range(2):
        for way in range(2):
            rs(way, 0, h).wait_recv()
        out[:, h * HALF : (h + 1) * HALF] = (
            own[h] + rs_in[0, 0, h].astype(F32) + rs_in[1, 0, h].astype(F32)
        ).astype(BF)

    for i, (src, dst) in enumerate(weights):
        remote(src, dst, w_send.at[i], w_recv.at[i], partner).wait_send()
    remote(several, several, meta_send, meta_recv, z_peer(1)).wait_send()
    remote(some, some, tot_send, tot_recv, x_peer(1)).wait_send()
    for g in range(4):
        for h in range(2):
            exchanged(sbuf, rbuf, d_send, d_recv, g, h).wait_send()
            exchanged(obuf, ybuf, r_send, r_recv, g, h).wait_send()
            for way in range(2):
                if g < 3 or way == h:
                    ag(way, g + 1, h).wait_send()
                    rs(way, g, h).wait_send()


def on_device(tokens, expert_ids, route_probs, shard_limit, gate_proj, up_proj, down_proj):
    dma = pltpu.SemaphoreType.DMA
    anywhere = pl.BlockSpec(memory_space=pl.ANY)
    near = pl.BlockSpec(memory_space=pltpu.VMEM)
    return pl.pallas_call(
        kernel,
        out_shape=jax.ShapeDtypeStruct((TOK, WIDTH), BF),
        in_specs=[anywhere, near, near, near, anywhere, anywhere, anywhere],
        out_specs=near,
        scratch_shapes=[
            pltpu.VMEM((NZ, 2, TOK, HALF), BF),
            pltpu.VMEM((NZ, 2 * SLOTS, EXPERTS), F32),
            pltpu.VMEM((NX, 8, EXPERTS), F32),
            pltpu.VMEM((WIDTH, HIDDEN), BF),
            pltpu.VMEM((WIDTH, HIDDEN), BF),
            pltpu.VMEM((HIDDEN, WIDTH), BF),
            pltpu.VMEM((4, 2, ROWS, HALF), BF),
            pltpu.VMEM((4, 2, ROWS, HALF), BF),
            pltpu.VMEM((ROWS, HIDDEN), BF),
            pltpu.VMEM((4, 2, ROWS, HALF), BF),
            pltpu.VMEM((4, 2, ROWS, HALF), BF),
            pltpu.VMEM((4, 2 * TOK, ROWS), BF),
            pltpu.VMEM((2 * TOK, HALF), F32),
            pltpu.VMEM((2, TOK, HALF), F32),
            pltpu.VMEM((2, 4, 2, TOK, HALF), BF),
            pltpu.VMEM((2, 4, 2, TOK, HALF), BF),
            dma((2,)), dma((3,)), dma((3,)), dma((3,)), dma, dma, dma, dma,
            dma((2, 4, 2)), dma((2, 4, 2)), dma((4, 2)), dma((4, 2)), dma((4, 2)), dma((4, 2)),
            dma((2, 4, 2)), dma((2, 4, 2)),
        ],
        compiler_params=pltpu.CompilerParams(
            collective_id=0, has_side_effects=True, vmem_limit_bytes=60 * 1024 * 1024
        ),
        name="expert_layer",
    )(tokens, expert_ids, route_probs, shard_limit, gate_proj, up_proj, down_proj)


def solution(mesh):
    whole = ("dp", "expert")
    in_specs = (
        P(whole, None), P(whole, None), P(whole, None), P(whole, None),
        P(whole, None, None), P(whole, None, None), P(whole, None, None),
    )
    return jax.shard_map(
        on_device, mesh=mesh, in_specs=in_specs, out_specs=P(whole, None), check_vma=False
    )
```

profile of v0, /device:TPU:4, one launch (start us, length us, event | category | flops | bytes accessed | tf_op | source)
XLA Modules:
  0.0 147.4 jit_solution(3497891538296441025)
XLA Ops:
  0.0 1.4 copy.8.ids
  1.4 1.4 copy.9.probs
  2.8 142.6 %expert_layer.1 = bf16[128,2048]{1,0:T(8,128)(2,1)} custom-call(bf16[128,2048]{1,0:T(8,128)(2,1)} %tokens.1, s32[128,8]{1,0:T(8,128)} %copy.8.ids, f32[128,8]{1,0:T(8,128)} %copy.9.probs, s32[1,128]{1,0:T(1,128)} %limit.1, bf16[1,2048,384]{2,1,0:T(8,128)(2,1)} %gate.1, bf16[1,2048,384]{2,1,0:T(8,128)(2,1)} %up.1, bf16[1,384,2048]{2,1,0:T(8,128)(2,1)} %down.1), custom_call_target="tpu_custom_call" | custom-call | tf_op jit(solution)/shard_map/expert_layer/pallas_call | solution.py:330
  145.5 1.9 %copy.11 = bf16[128,2048]{1,0:T(8,128)(2,1)} copy(bf16[128,2048]{1,0:T(8,128)(2,1)} %expert_layer.1) | data formatting | bytes 1048576
where the time goes:
time: 148 us; the launch traced here: 147 us
  Pallas kernels  143 us (97%)
  local copies, waits for them, and re-layouts  4.7 us (3%)
    pallas_call x1, Pallas kernels, on_device(): pl.pallas_call(kernel, out_shape=jax.ShapeDtypeStruct((TOK, WIDTH), BF),...  143 us
    unnamed x3, local copies, waits for them, and re-layouts  4.7 us

commit v1 on v0

v1 whole, which is shorter than its diff:
```python
import jax
import jax.numpy as jnp
from jax import lax
from jax.experimental import pallas as pl
from jax.experimental.pallas import tpu as pltpu
from jax.sharding import PartitionSpec as P

MESH = pl.DeviceIdType.MESH
BF = jnp.bfloat16
F32 = jnp.float32

NX, NY, NZ = 4, 4, 8
TOK = 128
SLOTS = 8
COL_CAP = 128
WIDTH = 2048
CHUNKS = 4
COLS = WIDTH // CHUNKS
HIDDEN = 768
PEERS = NX * NY
UNIT = 2 * SLOTS
ROWS = PEERS * UNIT
EXPERTS = 128
FAR = NZ // 2
UP, DOWN = 0, 1


def kernel(
    tokens, ids, probs, limit, gate, up, down, out,
    tok, meta, totals, gw, uw, dw, sbuf, rbuf, hid, obuf, ybuf, mix, part, rs_in, rs_out,
    in_sem, w_loc, w_send, w_recv, meta_send, meta_recv, tot_send, tot_recv,
    ag_send, ag_recv, d_send, d_recv, r_send, r_recv, rs_send, rs_recv,
):
    d = lax.axis_index("dp")
    c_all = lax.axis_index("expert")
    x, z = d // NZ, d % NZ
    y, core = c_all // 2, c_all % 2
    me = x * NY + y
    partner = (d, y * 2 + (1 - core))

    def z_peer(step):
        return (x * NZ + (z + step) % NZ, c_all)

    def neighbour(way):
        return z_peer(1 if way == UP else NZ - 1)

    def xy_peer(i):
        px, py = (x + i % NX) % NX, (y + i // NX) % NY
        return px * NY + py, (px * NZ + z, py * 2 + core)

    def x_peer(i):
        return (((x + i) % NX) * NZ + z, c_all)

    def rows_of(chip):
        return pl.ds(pl.multiple_of(chip * UNIT, UNIT), UNIT)

    def remote(src, dst, send, recv, device):
        return pltpu.make_async_remote_copy(
            src_ref=src, dst_ref=dst, send_sem=send, recv_sem=recv,
            device_id=device, device_id_type=MESH,
        )

    def own_tokens(c):
        return pltpu.make_async_copy(tokens.at[:, pl.ds(c * COLS, COLS)], tok.at[z, c], in_sem.at[c])

    for c in range(CHUNKS):
        own_tokens(c).start()
    wide = pl.ds(pl.multiple_of(core * (HIDDEN // 2), HIDDEN // 2), HIDDEN // 2)
    other = pl.ds(pl.multiple_of((1 - core) * (HIDDEN // 2), HIDDEN // 2), HIDDEN // 2)
    weights = (
        (gate.at[0], gw.at[:, wide]), (up.at[0], uw.at[:, wide]), (down.at[0], dw.at[wide, :]),
    )
    theirs = (gw.at[:, other], uw.at[:, other], dw.at[other, :])
    for i, (src, dst) in enumerate(weights):
        pltpu.make_async_copy(src, dst, w_loc.at[i]).start()

    barrier = pltpu.get_barrier_semaphore()
    pl.semaphore_signal(barrier, inc=1, device_id=partner, device_id_type=MESH)

    def greet_z(i, carry):
        pl.semaphore_signal(barrier, inc=1, device_id=z_peer(i), device_id_type=MESH)
        return carry

    def greet_xy(i, carry):
        pl.semaphore_signal(barrier, inc=1, device_id=xy_peer(i)[1], device_id_type=MESH)
        return carry

    lax.fori_loop(1, NZ, greet_z, 0)
    lax.fori_loop(1, PEERS, greet_xy, 0)

    col = lax.broadcasted_iota(jnp.int32, (EXPERTS, TOK), 1)
    row = lax.broadcasted_iota(jnp.int32, (EXPERTS, TOK), 0)
    chosen = jnp.zeros((EXPERTS, TOK), F32)
    weight = jnp.zeros((EXPERTS, TOK), F32)
    for k in range(8):
        hit = ids[k : k + 1, :] == row
        chosen = jnp.where(hit, 1.0, chosen)
        weight = jnp.where(hit, probs[k : k + 1, :], weight)
    earlier = jnp.where(row < col, 1.0, 0.0).astype(BF)
    rank = jnp.dot(chosen.astype(BF), earlier, preferred_element_type=F32)
    rank = jnp.where(chosen > 0.5, rank, 1000.0).T
    weight = weight.T
    rank = jnp.where(rank < limit[...].astype(F32), rank, 1000.0)
    token_id = row.astype(F32)
    for r in range(SLOTS):
        at = rank == float(r)
        meta[z, r : r + 1, :] = jnp.sum(jnp.where(at, token_id + 1000.0, 0.0), axis=0, keepdims=True) - 1000.0
        meta[z, SLOTS + r : SLOTS + r + 1, :] = jnp.sum(jnp.where(at, weight, 0.0), axis=0, keepdims=True)

    pl.semaphore_wait(barrier, NZ - 1 + PEERS - 1 + 1)

    def send_meta(i, carry):
        remote(meta.at[z], meta.at[z], meta_send, meta_recv, z_peer(i)).start()
        return carry

    lax.fori_loop(1, NZ, send_meta, 0)

    def ag(way, hop, c):
        block = (z + NZ - hop + 1) % NZ if way == UP else (z + hop - 1) % NZ
        return remote(
            tok.at[block, c], tok.at[block, c], ag_send.at[way, hop - 1, c], ag_recv.at[way, hop - 1, c],
            neighbour(way),
        )

    def ag_arrival(way, hop, c):
        block = (z + NZ - hop) % NZ if way == UP else (z + hop) % NZ
        return remote(
            tok.at[block, c], tok.at[block, c], ag_send.at[way, hop - 1, c], ag_recv.at[way, hop - 1, c],
            neighbour(way),
        )

    for c in range(CHUNKS):
        own_tokens(c).wait()
        for way in range(2):
            ag(way, 1, c).start()
    for i, (src, dst) in enumerate(weights):
        remote(src, dst, w_send.at[i], w_recv.at[i], partner).start()

    def metas():
        several = meta.at[pl.ds(0, NZ - 1)]
        return remote(several, several, meta_send, meta_recv, z_peer(1))

    def some_totals():
        some = totals.at[pl.ds(0, NX - 1)]
        return remote(some, some, tot_send, tot_recv, x_peer(1))

    def count_of(s):
        return jnp.sum(jnp.where(meta[s, 0:SLOTS, :] >= 0.0, 1.0, 0.0), axis=0, keepdims=True)

    def send_totals():
        total = jnp.zeros((1, EXPERTS), F32)
        for s in range(NZ):
            total = total + count_of(s)
        totals[x] = jnp.broadcast_to(total, (8, EXPERTS))

        def send_total(i, carry):
            remote(totals.at[x], totals.at[x], tot_send, tot_recv, x_peer(i)).start()
            return carry

        lax.fori_loop(1, NX, send_total, 0)

    def pair(k):
        return (z + NZ - k) % NZ, (z + k) % NZ

    def far_chunk(k, c):
        return c + 2 * (1 - (k % 4 + 3) // 4)

    def slot_values(first, second):
        stacked = jnp.concatenate([first, second] * PEERS, axis=0)
        s = lax.broadcasted_iota(jnp.int32, (ROWS, EXPERTS), 0)
        e = lax.broadcasted_iota(jnp.int32, (ROWS, EXPERTS), 1)
        chip = s >> 4
        expert = (chip >> 2) * (NZ * NY) + z * NY + (chip & 3)
        return jnp.sum(jnp.where(e == expert, stacked, 0.0), axis=1, keepdims=True)

    def selection(k):
        a, b = pair(k)
        source = slot_values(meta[a, 0:SLOTS, :], meta[b, 0:SLOTS, :])
        s = lax.broadcasted_iota(jnp.int32, (ROWS, 2 * TOK), 0)
        t = lax.broadcasted_iota(jnp.int32, (ROWS, 2 * TOK), 1)
        second = (s >> 3) & 1
        return (t - second * TOK).astype(F32) == source

    def exchange(src, dst, send, recv, k, c):
        def one(i, carry):
            chip, device = xy_peer(i)
            remote(src.at[k, c, rows_of(chip)], dst.at[k, c, rows_of(me)], send.at[k, c], recv.at[k, c], device).start()
            return carry

        lax.fori_loop(1, PEERS, one, 0)

    def exchanged(src, dst, send, recv, k, c):
        most = pl.ds(0, (PEERS - 1) * UNIT)
        return remote(src.at[k, c, most], dst.at[k, c, most], send.at[k, c], recv.at[k, c], x_peer(1))

    def dispatch(k, c):
        a, b = pair(k)
        c_b = far_chunk(k, c)

        def arrive_up():
            ag_arrival(UP, k, c).wait_recv()

        def arrive_down():
            ag_arrival(DOWN, k, c_b).wait_recv()

        if c < 2:
            pl.when(k > 0)(arrive_up)
            pl.when((k > 0) & (k < FAR))(lambda: ag(UP, k + 1, c).start())
            pl.when(k > 0)(arrive_down)
            pl.when((k > 0) & (k < FAR - 1))(lambda: ag(DOWN, k + 1, c).start())
        else:
            arrive_up()
            pl.when(k < FAR - 1)(lambda: ag(UP, k + 1, c).start())
            arrive_down()
            ag(DOWN, k + 1, c).start()
        both = jnp.concatenate([tok[a, c], tok[b, c_b]], axis=0)
        sbuf[k, c] = jnp.dot(mix[k], both, preferred_element_type=F32).astype(BF)
        exchange(sbuf, rbuf, d_send, d_recv, k, c)
        rbuf[k, c, rows_of(me), :] = sbuf[k, c, rows_of(me), :]

    second_half = (lax.broadcasted_iota(jnp.int32, (ROWS, 256), 0) >> 3) & 1
    second_wide = (lax.broadcasted_iota(jnp.int32, (ROWS, COLS), 0) >> 3) & 1

    def block(c):
        return slice(c * COLS, (c + 1) * COLS)

    def split_k(k):
        return (k > 0) & (k < FAR)

    def hidden(k, n):
        cols = slice(n * 256, (n + 1) * 256)

        def product(chunk, w, rows):
            return jnp.dot(rbuf[k, chunk], w[block(rows), cols], preferred_element_type=F32)

        def finish(gv, uv):
            hid[:, cols] = (gv / (1.0 + jnp.exp(-gv)) * uv).astype(BF)

        @pl.when(split_k(k))
        def _():
            finish(*(sum(product(c, w, c) for c in range(CHUNKS)) for w in (gw, uw)))

        @pl.when(jnp.logical_not(split_k(k)))
        def _():
            sums = []
            for w in (gw, uw):
                left = product(0, w, 0) + product(1, w, 1)
                right = product(0, w, 2) + product(1, w, 3)
                half = jnp.where(second_half == 0, left, right)
                swapped = jnp.where(
                    second_half == 0, pltpu.roll(half, ROWS - SLOTS, 0), pltpu.roll(half, SLOTS, 0)
                )
                sums.append(half + swapped)
            finish(*sums)

    def wait_rows(k):
        for c in range(2):
            exchanged(sbuf, rbuf, d_send, d_recv, k, c).wait_recv()

        @pl.when(split_k(k))
        def _():
            for c in range(2, CHUNKS):
                exchanged(sbuf, rbuf, d_send, d_recv, k, c).wait_recv()

    def outputs(k):
        def product(c):
            return jnp.dot(hid[...], dw[:, block(c)], preferred_element_type=F32)

        def keep(c, value):
            obuf[k, c] = value.astype(BF)
            ybuf[k, c, rows_of(me), :] = obuf[k, c, rows_of(me), :]

        @pl.when(split_k(k))
        def _():
            for c in range(CHUNKS):
                keep(c, product(c))

        @pl.when(jnp.logical_not(split_k(k)))
        def _():
            for c in range(2):
                keep(c, jnp.where(second_wide == 0, product(c), product(c + 2)))

    def weights_here():
        for i, (src, dst) in enumerate(weights):
            pltpu.make_async_copy(src, dst, w_loc.at[i]).wait()
            remote(src, theirs[i], w_send.at[i], w_recv.at[i], partner).wait_recv()

    def send_back(k):
        for c in range(2):
            exchange(obuf, ybuf, r_send, r_recv, k, c)

        @pl.when(split_k(k))
        def _():
            for c in range(2, CHUNKS):
                exchange(obuf, ybuf, r_send, r_recv, k, c)

    def weigh_all():
        some_totals().wait_recv()
        before_x = jnp.zeros((1, EXPERTS), F32)
        for s in range(NX):
            before_x = before_x + jnp.where(s < x, 1.0, 0.0) * totals[s, 0:1, :]

        def kept_weight(shard):
            offset = before_x
            for s in range(NZ):
                offset = offset + jnp.where(s < shard, 1.0, 0.0) * count_of(s)
            r = lax.broadcasted_iota(jnp.int32, (SLOTS, EXPERTS), 0).astype(F32)
            return jnp.where(offset + r < float(COL_CAP), meta[shard, SLOTS : 2 * SLOTS, :], 0.0)

        def weigh(k, carry):
            a, b = pair(k)
            w = slot_values(kept_weight(a), kept_weight(b))
            mix[k] = jnp.where(selection(k), w, 0.0).T.astype(BF)
            return carry

        lax.fori_loop(0, FAR + 1, weigh, 0)

    def step(k, carry):
        @pl.when(k == 1)
        def _():
            metas().wait_recv()
            send_totals()

        @pl.when(k <= FAR)
        def _():
            mix[k] = jnp.where(selection(k), 1.0, 0.0).astype(BF)

        for c in range(CHUNKS):
            if c < 2:
                pl.when(k <= FAR)(lambda: dispatch(k, c))
            else:
                pl.when(split_k(k))(lambda: dispatch(k, c))
            if c == 0:
                pl.when(k > 1)(lambda: hidden(k - 2, 2))
            if c == 1:
                pl.when(k > 1)(lambda: outputs(k - 2))
            if c == 2:
                pl.when(k == FAR + 1)(weigh_all)
                pl.when(k == 1)(weights_here)

                @pl.when((k > 0) & (k < FAR + 2))
                def _():
                    wait_rows(k - 1)
                    hidden(k - 1, 0)

            if c == 3:
                pl.when((k > 0) & (k < FAR + 2))(lambda: hidden(k - 1, 1))
        return carry

    lax.fori_loop(0, FAR + 3, step, 0)
    send_back(FAR)

    def rs(way, k, c):
        return remote(
            rs_out.at[way, k - 1, c], rs_in.at[way, k - 1, c], rs_send.at[way, k - 1, c], rs_recv.at[way, k - 1, c],
            neighbour(way),
        )

    def gather_part(k, c):
        exchanged(obuf, ybuf, r_send, r_recv, k, c).wait_recv()
        part[...] = jnp.dot(mix[k], ybuf[k, c], preferred_element_type=F32)

    def collect(i, carry):
        k = FAR - i
        send_back(k - 1)

        @pl.when(k == FAR)
        def _():
            for c in range(2):
                gather_part(k, c)
                for way in range(2):
                    rs_out[way, FAR - 1, c + 2 * way] = part[way * TOK : (way + 1) * TOK, :].astype(BF)
                    rs(way, FAR, c + 2 * way).start()

        @pl.when(k < FAR)
        def _():
            for c in range(CHUNKS):
                gather_part(k, c)
                for way in range(2):
                    mine = slice(TOK, 2 * TOK) if way == UP else slice(0, TOK)

                    def add(way=way, mine=mine):
                        rs(way, k + 1, c).wait_recv()
                        rs_out[way, k - 1, c] = (part[mine, :] + rs_in[way, k, c].astype(F32)).astype(BF)

                    def first(way=way, mine=mine):
                        rs_out[way, k - 1, c] = part[mine, :].astype(BF)

                    if c // 2 == way:
                        add()
                    else:
                        pl.when(k < FAR - 1)(add)
                        pl.when(k == FAR - 1)(first)
                    rs(way, k, c).start()

        return carry

    lax.fori_loop(0, FAR, collect, 0)

    for c in range(2):
        gather_part(0, c)
        for q in range(2):
            chunk = c + 2 * q
            for way in range(2):
                rs(way, 1, chunk).wait_recv()
            out[:, block(chunk)] = (
                part[q * TOK : (q + 1) * TOK, :] + rs_in[UP, 0, chunk].astype(F32) + rs_in[DOWN, 0, chunk].astype(F32)
            ).astype(BF)

    for i, (src, dst) in enumerate(weights):
        remote(src, dst, w_send.at[i], w_recv.at[i], partner).wait_send()
    metas().wait_send()
    some_totals().wait_send()
    for k in range(FAR + 1):
        for c in range(CHUNKS if 0 < k < FAR else 2):
            exchanged(sbuf, rbuf, d_send, d_recv, k, c).wait_send()
            exchanged(obuf, ybuf, r_send, r_recv, k, c).wait_send()
    for hop in range(1, FAR + 1):
        for c in range(CHUNKS):
            for way in range(2):
                if hop < FAR or c // 2 == way:
                    ag(way, hop, c).wait_send()
                    rs(way, hop, c).wait_send()


def on_device(tokens, expert_ids, route_probs, shard_limit, gate_proj, up_proj, down_proj):
    dma = pltpu.SemaphoreType.DMA
    anywhere = pl.BlockSpec(memory_space=pltpu.HBM)
    near = pl.BlockSpec(memory_space=pltpu.VMEM)
    unit = (FAR + 1, CHUNKS, ROWS, COLS)
    ring = (2, FAR, CHUNKS)
    return pl.pallas_call(
        kernel,
        out_shape=jax.ShapeDtypeStruct((TOK, WIDTH), BF),
        in_specs=[anywhere, near, near, near, anywhere, anywhere, anywhere],
        out_specs=near,
        scratch_shapes=[
            pltpu.VMEM((NZ, CHUNKS, TOK, COLS), BF),
            pltpu.VMEM((NZ, 2 * SLOTS, EXPERTS), F32),
            pltpu.VMEM((NX, 8, EXPERTS), F32),
            pltpu.VMEM((WIDTH, HIDDEN), BF),
            pltpu.VMEM((WIDTH, HIDDEN), BF),
            pltpu.VMEM((HIDDEN, WIDTH), BF),
            pltpu.VMEM(unit, BF),
            pltpu.VMEM(unit, BF),
            pltpu.VMEM((ROWS, HIDDEN), BF),
            pltpu.VMEM(unit, BF),
            pltpu.VMEM(unit, BF),
            pltpu.VMEM((FAR + 1, 2 * TOK, ROWS), BF),
            pltpu.VMEM((2 * TOK, COLS), F32),
            pltpu.VMEM((*ring, TOK, COLS), BF),
            pltpu.VMEM((*ring, TOK, COLS), BF),
            dma((CHUNKS,)), dma((3,)), dma((3,)), dma((3,)), dma, dma, dma, dma,
            dma(ring), dma(ring),
            dma(unit[:2]), dma(unit[:2]), dma(unit[:2]), dma(unit[:2]),
            dma(ring), dma(ring),
        ],
        compiler_params=pltpu.CompilerParams(
            collective_id=0, has_side_effects=True, vmem_limit_bytes=60000000
        ),
        name="expert_layer",
    )(tokens, expert_ids.T, route_probs.T, shard_limit, gate_proj, up_proj, down_proj)


def solution(mesh):
    whole = ("dp", "expert")
    in_specs = (
        P(whole, None), P(whole, None), P(whole, None), P(whole, None),
        P(whole, None, None), P(whole, None, None), P(whole, None, None),
    )
    return jax.shard_map(
        on_device, mesh=mesh, in_specs=in_specs, out_specs=P(whole, None), check_vma=False
    )
```

time: 148 us -> 116 us (0.78)
  Pallas kernels: 143 us -> 113 us
  local copies, waits for them, and re-layouts: 4.7 us -> 1.88 us
    pallas_call x1, Pallas kernels: 143 us -> 113 us  [on_device(): pl.pallas_call(kernel, out_shape=jax.ShapeDtypeStruct((TOK, WIDTH), BF),...]
    unnamed x3 -> x1, local copies, waits for them, and re-layouts: 4.7 us -> 1.88 us
where the time goes in v1:
time: 116 us; the launch traced here: 115 us
  Pallas kernels  113 us (97%)
  local copies, waits for them, and re-layouts  1.88 us (2%)
    pallas_call x1, Pallas kernels, on_device(): pl.pallas_call(kernel, out_shape=jax.ShapeDtypeStruct((TOK, WIDTH), BF),...  113 us

profile of v1, /device:TPU:4, one launch (start us, length us, event | category | flops | bytes accessed | tf_op | source)
XLA Modules:
  0.0 115.1 jit_solution(18003890355087088097)
XLA Ops:
  0.0 113.2 %expert_layer.1 = bf16[128,2048]{1,0:T(8,128)(2,1)} custom-call(bf16[128,2048]{1,0:T(8,128)(2,1)} %tokens.1, s32[8,128]{1,0:T(8,128)} %bitcast.2, f32[8,128]{1,0:T(8,128)} %bitcast.3, s32[1,128]{1,0:T(1,128)} %limit.1, bf16[1,2048,384]{2,1,0:T(8,128)(2,1)} %gate.1, bf16[1,2048,384]{2,1,0:T(8,128)(2,1)} %up.1, bf16[1,384,2048]{2,1,0:T(8,128)(2,1)} %down.1), custom_call_target="tpu_custom_call" | custom-call | tf_op jit(solution)/shard_map/expert_layer/pallas_call | solution.py:432
  113.2 1.9 %copy.9 = bf16[128,2048]{1,0:T(8,128)(2,1)} copy(bf16[128,2048]{1,0:T(8,128)(2,1)} %expert_layer.1) | data formatting | bytes 1048576

commit v2 on v1

--- a/solution.py
+++ b/solution.py
@@ -27,7 +27,7 @@
 
 def kernel(
     tokens, ids, probs, limit, gate, up, down, out,
-    tok, meta, totals, gw, uw, dw, sbuf, rbuf, hid, obuf, ybuf, mix, part, rs_in, rs_out,
+    tok, meta, totals, gw, uw, dw, sbuf, rbuf, hid, obuf, ybuf, mix, part, held, rs_in, rs_out,
     in_sem, w_loc, w_send, w_recv, meta_send, meta_recv, tot_send, tot_recv,
     ag_send, ag_recv, d_send, d_recv, r_send, r_recv, rs_send, rs_recv,
 ):
@@ -107,13 +107,10 @@
         meta[z, r : r + 1, :] = jnp.sum(jnp.where(at, token_id + 1000.0, 0.0), axis=0, keepdims=True) - 1000.0
         meta[z, SLOTS + r : SLOTS + r + 1, :] = jnp.sum(jnp.where(at, weight, 0.0), axis=0, keepdims=True)
 
-    pl.semaphore_wait(barrier, NZ - 1 + PEERS - 1 + 1)
-
     def send_meta(i, carry):
         remote(meta.at[z], meta.at[z], meta_send, meta_recv, z_peer(i)).start()
         return carry
 
-    lax.fori_loop(1, NZ, send_meta, 0)
 
     def ag(way, hop, c):
         block = (z + NZ - hop + 1) % NZ if way == UP else (z + hop - 1) % NZ
@@ -128,13 +125,6 @@
             tok.at[block, c], tok.at[block, c], ag_send.at[way, hop - 1, c], ag_recv.at[way, hop - 1, c],
             neighbour(way),
         )
-
-    for c in range(CHUNKS):
-        own_tokens(c).wait()
-        for way in range(2):
-            ag(way, 1, c).start()
-    for i, (src, dst) in enumerate(weights):
-        remote(src, dst, w_send.at[i], w_recv.at[i], partner).start()
 
     def metas():
         several = meta.at[pl.ds(0, NZ - 1)]
@@ -193,8 +183,13 @@
         most = pl.ds(0, (PEERS - 1) * UNIT)
         return remote(src.at[k, c, most], dst.at[k, c, most], send.at[k, c], recv.at[k, c], x_peer(1))
 
+    def pick_rows(k, c):
+        a, b = pair(k)
+        both = jnp.concatenate([tok[a, c], tok[b, far_chunk(k, c)]], axis=0)
+        sbuf[k, c] = jnp.dot(mix[k], both, preferred_element_type=F32).astype(BF)
+        rbuf[k, c, rows_of(me), :] = sbuf[k, c, rows_of(me), :]
+
     def dispatch(k, c):
-        a, b = pair(k)
         c_b = far_chunk(k, c)
 
         def arrive_up():
@@ -204,19 +199,17 @@
             ag_arrival(DOWN, k, c_b).wait_recv()
 
         if c < 2:
-            pl.when(k > 0)(arrive_up)
-            pl.when((k > 0) & (k < FAR))(lambda: ag(UP, k + 1, c).start())
-            pl.when(k > 0)(arrive_down)
-            pl.when((k > 0) & (k < FAR - 1))(lambda: ag(DOWN, k + 1, c).start())
+            arrive_up()
+            pl.when(k < FAR)(lambda: ag(UP, k + 1, c).start())
+            arrive_down()
+            pl.when(k < FAR - 1)(lambda: ag(DOWN, k + 1, c).start())
         else:
             arrive_up()
             pl.when(k < FAR - 1)(lambda: ag(UP, k + 1, c).start())
             arrive_down()
             ag(DOWN, k + 1, c).start()
-        both = jnp.concatenate([tok[a, c], tok[b, c_b]], axis=0)
-        sbuf[k, c] = jnp.dot(mix[k], both, preferred_element_type=F32).astype(BF)
+        pick_rows(k, c)
         exchange(sbuf, rbuf, d_send, d_recv, k, c)
-        rbuf[k, c, rows_of(me), :] = sbuf[k, c, rows_of(me), :]
 
     second_half = (lax.broadcasted_iota(jnp.int32, (ROWS, 256), 0) >> 3) & 1
     second_wide = (lax.broadcasted_iota(jnp.int32, (ROWS, COLS), 0) >> 3) & 1
@@ -334,21 +327,46 @@
                 pl.when(k > 1)(lambda: hidden(k - 2, 2))
             if c == 1:
                 pl.when(k > 1)(lambda: outputs(k - 2))
+
+                @pl.when(k == FAR + 1)
+                def _():
+                    for early in (0, 2):
+                        exchange(obuf, ybuf, r_send, r_recv, FAR - 1, early)
+
             if c == 2:
                 pl.when(k == FAR + 1)(weigh_all)
                 pl.when(k == 1)(weights_here)
 
-                @pl.when((k > 0) & (k < FAR + 2))
+                @pl.when(k < FAR + 2)
                 def _():
                     wait_rows(k - 1)
                     hidden(k - 1, 0)
 
             if c == 3:
-                pl.when((k > 0) & (k < FAR + 2))(lambda: hidden(k - 1, 1))
+                pl.when(k < FAR + 2)(lambda: hidden(k - 1, 1))
         return carry
 
-    lax.fori_loop(0, FAR + 3, step, 0)
-    send_back(FAR)
+    for c in range(CHUNKS):
+        own_tokens(c).wait()
+    mix[0] = jnp.where(selection(0), 1.0, 0.0).astype(BF)
+    for c in range(2):
+        pick_rows(0, c)
+
+    pl.semaphore_wait(barrier, NZ - 1 + PEERS - 1 + 1)
+    lax.fori_loop(1, NZ, send_meta, 0)
+    for c in range(CHUNKS):
+        for way in range(2):
+            ag(way, 1, c).start()
+        if c < 2:
+            exchange(sbuf, rbuf, d_send, d_recv, 0, c)
+    for i, (src, dst) in enumerate(weights):
+        remote(src, dst, w_send.at[i], w_recv.at[i], partner).start()
+
+    lax.fori_loop(1, FAR + 3, step, 0)
+    for c in (0, 1):
+        exchange(obuf, ybuf, r_send, r_recv, FAR, c)
+    for c in (1, 3):
+        exchange(obuf, ybuf, r_send, r_recv, FAR - 1, c)
 
     def rs(way, k, c):
         return remote(
@@ -360,42 +378,72 @@
         exchanged(obuf, ybuf, r_send, r_recv, k, c).wait_recv()
         part[...] = jnp.dot(mix[k], ybuf[k, c], preferred_element_type=F32)
 
+    def mine(way):
+        return slice(TOK, 2 * TOK) if way == UP else slice(0, TOK)
+
+    def begin(c):
+        gather_part(FAR - 1, c)
+        later = c // 2
+        rs_out[1 - later, FAR - 2, c] = part[mine(1 - later), :].astype(BF)
+        rs(1 - later, FAR - 1, c).start()
+        held[c] = part[mine(later), :]
+
+    def flush(c):
+        later = c // 2
+        rs(later, FAR, c).wait_recv()
+        rs_out[later, FAR - 2, c] = (held[c] + rs_in[later, FAR - 1, c].astype(F32)).astype(BF)
+        rs(later, FAR - 1, c).start()
+
+    def begin_far(c):
+        gather_part(FAR, c)
+        for way in range(2):
+            rs_out[way, FAR - 1, c + 2 * way] = part[way * TOK : (way + 1) * TOK, :].astype(BF)
+            rs(way, FAR, c + 2 * way).start()
+
+    send_back(FAR - 2)
+    begin(0)
+    begin(2)
+    begin_far(0)
+    begin_far(1)
+    begin(1)
+    flush(0)
+    flush(2)
+    begin(3)
+    flush(1)
+    flush(3)
+    for k in (0, FAR):
+        for c in range(2):
+            exchanged(sbuf, rbuf, d_send, d_recv, k, c).wait_send()
+
     def collect(i, carry):
-        k = FAR - i
+        k = FAR - 2 - i
         send_back(k - 1)
-
-        @pl.when(k == FAR)
-        def _():
-            for c in range(2):
-                gather_part(k, c)
-                for way in range(2):
-                    rs_out[way, FAR - 1, c + 2 * way] = part[way * TOK : (way + 1) * TOK, :].astype(BF)
-                    rs(way, FAR, c + 2 * way).start()
-
-        @pl.when(k < FAR)
-        def _():
-            for c in range(CHUNKS):
-                gather_part(k, c)
-                for way in range(2):
-                    mine = slice(TOK, 2 * TOK) if way == UP else slice(0, TOK)
-
-                    def add(way=way, mine=mine):
-                        rs(way, k + 1, c).wait_recv()
-                        rs_out[way, k - 1, c] = (part[mine, :] + rs_in[way, k, c].astype(F32)).astype(BF)
-
-                    def first(way=way, mine=mine):
-                        rs_out[way, k - 1, c] = part[mine, :].astype(BF)
-
-                    if c // 2 == way:
-                        add()
-                    else:
-                        pl.when(k < FAR - 1)(add)
-                        pl.when(k == FAR - 1)(first)
-                    rs(way, k, c).start()
-
+        for c in range(CHUNKS):
+            gather_part(k, c)
+            for way in range(2):
+                rs(way, k + 1, c).wait_recv()
+                rs_out[way, k - 1, c] = (part[mine(way), :] + rs_in[way, k, c].astype(F32)).astype(BF)
+                rs(way, k, c).start()
+            exchanged(sbuf, rbuf, d_send, d_recv, k, c).wait_send()
+            exchanged(obuf, ybuf, r_send, r_recv, k + 1, c).wait_send()
+            for way in range(2):
+                ag(way, k, c).wait_send()
+                rs(way, k + 1, c).wait_send()
         return carry
 
-    lax.fori_loop(0, FAR, collect, 0)
+    lax.fori_loop(0, FAR - 2, collect, 0)
+    for i, (src, dst) in enumerate(weights):
+        remote(src, dst, w_send.at[i], w_recv.at[i], partner).wait_send()
+    metas().wait_send()
+    some_totals().wait_send()
+    for c in range(CHUNKS):
+        exchanged(sbuf, rbuf, d_send, d_recv, FAR - 1, c).wait_send()
+        for way in range(2):
+            ag(way, FAR - 1, c).wait_send()
+        ag(c // 2, FAR, c).wait_send()
+        rs(c // 2, FAR, c).wait_send()
+    for c in range(2):
+        exchanged(obuf, ybuf, r_send, r_recv, FAR, c).wait_send()
 
     for c in range(2):
         gather_part(0, c)
@@ -407,20 +455,12 @@
                 part[q * TOK : (q + 1) * TOK, :] + rs_in[UP, 0, chunk].astype(F32) + rs_in[DOWN, 0, chunk].astype(F32)
             ).astype(BF)
 
-    for i, (src, dst) in enumerate(weights):
-        remote(src, dst, w_send.at[i], w_recv.at[i], partner).wait_send()
-    metas().wait_send()
-    some_totals().wait_send()
-    for k in range(FAR + 1):
-        for c in range(CHUNKS if 0 < k < FAR else 2):
-            exchanged(sbuf, rbuf, d_send, d_recv, k, c).wait_send()
-            exchanged(obuf, ybuf, r_send, r_recv, k, c).wait_send()
-    for hop in range(1, FAR + 1):
-        for c in range(CHUNKS):
-            for way in range(2):
-                if hop < FAR or c // 2 == way:
-                    ag(way, hop, c).wait_send()
-                    rs(way, hop, c).wait_send()
+    for c in range(CHUNKS):
+        exchanged(obuf, ybuf, r_send, r_recv, 1, c).wait_send()
+        for way in range(2):
+            rs(way, 1, c).wait_send()
+    for c in range(2):
+        exchanged(obuf, ybuf, r_send, r_recv, 0, c).wait_send()
 
 
 def on_device(tokens, expert_ids, route_probs, shard_limit, gate_proj, up_proj, down_proj):
@@ -448,6 +488,7 @@
             pltpu.VMEM(unit, BF),
             pltpu.VMEM((FAR + 1, 2 * TOK, ROWS), BF),
             pltpu.VMEM((2 * TOK, COLS), F32),
+            pltpu.VMEM((CHUNKS, TOK, COLS), F32),
             pltpu.VMEM((*ring, TOK, COLS), BF),
             pltpu.VMEM((*ring, TOK, COLS), BF),
             dma((CHUNKS,)), dma((3,)), dma((3,)), dma((3,)), dma, dma, dma, dma,
@@ -456,7 +497,7 @@
             dma(ring), dma(ring),
         ],
         compiler_params=pltpu.CompilerParams(
-            collective_id=0, has_side_effects=True, vmem_limit_bytes=60000000
+            collective_id=0, has_side_effects=True, vmem_limit_bytes=56000000
         ),
         name="expert_layer",
     )(tokens, expert_ids.T, route_probs.T, shard_limit, gate_proj, up_proj, down_proj)

time: 116 us -> 113 us (0.974)
  Pallas kernels: 113 us -> 109 us
    pallas_call x1, Pallas kernels: 113 us -> 109 us  [on_device(): pl.pallas_call(kernel, out_shape=jax.ShapeDtypeStruct((TOK, WIDTH), BF),...]
    unnamed x1 -> x7, local copies, waits for them, and re-layouts: 1.88 us -> 2.82 us
where the time goes in v2:
time: 113 us; the launch traced here: 111 us
  Pallas kernels  109 us (96%)
  local copies, waits for them, and re-layouts  2.82 us (2%)
    pallas_call x1, Pallas kernels, on_device(): pl.pallas_call(kernel, out_shape=jax.ShapeDtypeStruct((TOK, WIDTH), BF),...  109 us
    unnamed x7, local copies, waits for them, and re-layouts  2.82 us

profile of v2, /device:TPU:4, one launch (start us, length us, event | category | flops | bytes accessed | tf_op | source)
XLA Modules:
  0.0 111.4 jit_solution(15596626467619104138)
XLA Ops:
  0.0 0.0 copy-start
  0.0 0.7 copy-done
  0.7 0.0 copy-start.1
  0.7 0.7 copy-done.1
  1.4 0.0 copy-start.2
  1.4 0.7 copy-done.2
  2.0 108.5 %expert_layer.1 = bf16[128,2048]{1,0:T(8,128)(2,1)S(1)} custom-call(bf16[128,2048]{1,0:T(8,128)(2,1)} %tokens.1, s32[8,128]{1,0:T(8,128)S(1)} %bitcast.2, f32[8,128]{1,0:T(8,128)S(1)} %bitcast.3, s32[1,128]{1,0:T(1,128)S(1)} %copy-done.2, bf16[1,2048,384]{2,1,0:T(8,128)(2,1)} %gate.1, bf16[1,2048,384]{2,1,0:T(8,128)(2,1)} %up.1, bf16[1,384,2048]{2,1,0:T(8,128)(2,1)} %down.1), custom_call_target="tpu_custom_call" | custom-call | tf_op jit(solution)/shard_map/expert_layer/pallas_call | solution.py:472
  110.6 0.8 copy.9
Async XLA Ops:
  0.0 0.7 copy-start
  0.7 0.7 copy-start.1
  1.4 0.7 copy-start.2

commit v3 on v2

--- a/solution.py
+++ b/solution.py
@@ -27,7 +27,7 @@
 
 def kernel(
     tokens, ids, probs, limit, gate, up, down, out,
-    tok, meta, totals, gw, uw, dw, sbuf, rbuf, hid, obuf, ybuf, mix, part, held, rs_in, rs_out,
+    tok, meta, totals, gw, uw, dw, sbuf, rbuf, gate_sum, up_sum, hid, obuf, ybuf, mix, part, rs_in, rs_out,
     in_sem, w_loc, w_send, w_recv, meta_send, meta_recv, tot_send, tot_recv,
     ag_send, ag_recv, d_send, d_recv, r_send, r_recv, rs_send, rs_recv,
 ):
@@ -71,9 +71,6 @@
         (gate.at[0], gw.at[:, wide]), (up.at[0], uw.at[:, wide]), (down.at[0], dw.at[wide, :]),
     )
     theirs = (gw.at[:, other], uw.at[:, other], dw.at[other, :])
-    for i, (src, dst) in enumerate(weights):
-        pltpu.make_async_copy(src, dst, w_loc.at[i]).start()
-
     barrier = pltpu.get_barrier_semaphore()
     pl.semaphore_signal(barrier, inc=1, device_id=partner, device_id_type=MESH)
 
@@ -220,58 +217,46 @@
     def split_k(k):
         return (k > 0) & (k < FAR)
 
-    def hidden(k, n):
-        cols = slice(n * 256, (n + 1) * 256)
-
-        def product(chunk, w, rows):
-            return jnp.dot(rbuf[k, chunk], w[block(rows), cols], preferred_element_type=F32)
-
-        def finish(gv, uv):
+    def arrived(k, c):
+        exchanged(sbuf, rbuf, d_send, d_recv, k, c).wait_recv()
+
+    def add_chunk(k, c, spread, fresh):
+        arrived(k, c)
+        for total, w in ((gate_sum, gw), (up_sum, uw)):
+            for n in range(0, HIDDEN, 256):
+                cols = slice(n, n + 256)
+                value = jnp.dot(rbuf[k, c], w[block(c), cols], preferred_element_type=F32)
+                if spread:
+                    right = jnp.dot(rbuf[k, c], w[block(c + 2), cols], preferred_element_type=F32)
+                    value = jnp.where(second_half == 0, value, right)
+                total[:, cols] = value if fresh else total[:, cols] + value
+
+    def activate(spread):
+        for n in range(0, HIDDEN, 256):
+            cols = slice(n, n + 256)
+            values = []
+            for total in (gate_sum, up_sum):
+                value = total[:, cols]
+                if spread:
+                    value = value + jnp.where(
+                        second_half == 0, pltpu.roll(value, ROWS - SLOTS, 0), pltpu.roll(value, SLOTS, 0)
+                    )
+                values.append(value)
+            gv, uv = values
             hid[:, cols] = (gv / (1.0 + jnp.exp(-gv)) * uv).astype(BF)
 
-        @pl.when(split_k(k))
-        def _():
-            finish(*(sum(product(c, w, c) for c in range(CHUNKS)) for w in (gw, uw)))
-
-        @pl.when(jnp.logical_not(split_k(k)))
-        def _():
-            sums = []
-            for w in (gw, uw):
-                left = product(0, w, 0) + product(1, w, 1)
-                right = product(0, w, 2) + product(1, w, 3)
-                half = jnp.where(second_half == 0, left, right)
-                swapped = jnp.where(
-                    second_half == 0, pltpu.roll(half, ROWS - SLOTS, 0), pltpu.roll(half, SLOTS, 0)
-                )
-                sums.append(half + swapped)
-            finish(*sums)
-
-    def wait_rows(k):
+    def outputs(k):
         for c in range(2):
-            exchanged(sbuf, rbuf, d_send, d_recv, k, c).wait_recv()
-
-        @pl.when(split_k(k))
-        def _():
-            for c in range(2, CHUNKS):
-                exchanged(sbuf, rbuf, d_send, d_recv, k, c).wait_recv()
-
-    def outputs(k):
-        def product(c):
-            return jnp.dot(hid[...], dw[:, block(c)], preferred_element_type=F32)
-
-        def keep(c, value):
-            obuf[k, c] = value.astype(BF)
+            left, right = (
+                jnp.dot(hid[...], dw[:, block(chunk)], preferred_element_type=F32) for chunk in (c, c + 2)
+            )
+            obuf[k, c] = jnp.where(second_wide == 0, left, right).astype(BF)
             ybuf[k, c, rows_of(me), :] = obuf[k, c, rows_of(me), :]
 
-        @pl.when(split_k(k))
-        def _():
-            for c in range(CHUNKS):
-                keep(c, product(c))
-
-        @pl.when(jnp.logical_not(split_k(k)))
-        def _():
-            for c in range(2):
-                keep(c, jnp.where(second_wide == 0, product(c), product(c + 2)))
+            @pl.when(split_k(k))
+            def _():
+                obuf[k, c + 2] = jnp.where(second_wide == 0, right, left).astype(BF)
+                ybuf[k, c + 2, rows_of(me), :] = obuf[k, c + 2, rows_of(me), :]
 
     def weights_here():
         for i, (src, dst) in enumerate(weights):
@@ -323,31 +308,43 @@
                 pl.when(k <= FAR)(lambda: dispatch(k, c))
             else:
                 pl.when(split_k(k))(lambda: dispatch(k, c))
-            if c == 0:
-                pl.when(k > 1)(lambda: hidden(k - 2, 2))
-            if c == 1:
-                pl.when(k > 1)(lambda: outputs(k - 2))
+            if c < 2:
+                pl.when((k > 1) & (k <= FAR))(lambda: add_chunk(k - 1, c + 1, False, False))
+            if c == 2:
+                @pl.when(k == 1)
+                def _():
+                    weights_here()
+                    add_chunk(0, 0, True, True)
+                    add_chunk(0, 1, True, False)
+                    activate(True)
+
+                @pl.when((k > 1) & (k <= FAR))
+                def _():
+                    add_chunk(k - 1, 3, False, False)
+                    activate(False)
 
                 @pl.when(k == FAR + 1)
                 def _():
-                    for early in (0, 2):
+                    add_chunk(FAR, 1, True, False)
+                    activate(True)
+
+            if c == 3:
+                outputs(k - 1)
+                pl.when(k < FAR)(lambda: add_chunk(k, 0, False, True))
+
+                @pl.when(k == FAR)
+                def _():
+                    for early in range(2):
                         exchange(obuf, ybuf, r_send, r_recv, FAR - 1, early)
-
-            if c == 2:
-                pl.when(k == FAR + 1)(weigh_all)
-                pl.when(k == 1)(weights_here)
-
-                @pl.when(k < FAR + 2)
-                def _():
-                    wait_rows(k - 1)
-                    hidden(k - 1, 0)
-
-            if c == 3:
-                pl.when(k < FAR + 2)(lambda: hidden(k - 1, 1))
+                    weigh_all()
+                    add_chunk(FAR, 0, True, True)
+
         return carry
 
     for c in range(CHUNKS):
         own_tokens(c).wait()
+    for i, (src, dst) in enumerate(weights):
+        pltpu.make_async_copy(src, dst, w_loc.at[i]).start()
     mix[0] = jnp.where(selection(0), 1.0, 0.0).astype(BF)
     for c in range(2):
         pick_rows(0, c)
@@ -362,10 +359,10 @@
     for i, (src, dst) in enumerate(weights):
         remote(src, dst, w_send.at[i], w_recv.at[i], partner).start()
 
-    lax.fori_loop(1, FAR + 3, step, 0)
+    lax.fori_loop(1, FAR + 2, step, 0)
     for c in (0, 1):
         exchange(obuf, ybuf, r_send, r_recv, FAR, c)
-    for c in (1, 3):
+    for c in (2, 3):
         exchange(obuf, ybuf, r_send, r_recv, FAR - 1, c)
 
     def rs(way, k, c):
@@ -381,18 +378,23 @@
     def mine(way):
         return slice(TOK, 2 * TOK) if way == UP else slice(0, TOK)
 
+    def chunk_of(way, c):
+        return (c + 2) % CHUNKS if way == UP else c
+
+    def pass_on(way, k, c):
+        chunk = chunk_of(way, c)
+        rs(way, k + 1, chunk).wait_recv()
+        rs_out[way, k - 1, chunk] = (part[mine(way), :] + rs_in[way, k, chunk].astype(F32)).astype(BF)
+        rs(way, k, chunk).start()
+
     def begin(c):
         gather_part(FAR - 1, c)
-        later = c // 2
-        rs_out[1 - later, FAR - 2, c] = part[mine(1 - later), :].astype(BF)
-        rs(1 - later, FAR - 1, c).start()
-        held[c] = part[mine(later), :]
-
-    def flush(c):
-        later = c // 2
-        rs(later, FAR, c).wait_recv()
-        rs_out[later, FAR - 2, c] = (held[c] + rs_in[later, FAR - 1, c].astype(F32)).astype(BF)
-        rs(later, FAR - 1, c).start()
+        for way in range(2):
+            if c < 2:
+                rs_out[way, FAR - 2, chunk_of(way, c)] = part[mine(way), :].astype(BF)
+                rs(way, FAR - 1, chunk_of(way, c)).start()
+            else:
+                pass_on(way, FAR - 1, c)
 
     def begin_far(c):
         gather_part(FAR, c)
@@ -402,15 +404,11 @@
 
     send_back(FAR - 2)
     begin(0)
-    begin(2)
+    begin(1)
     begin_far(0)
     begin_far(1)
-    begin(1)
-    flush(0)
-    flush(2)
+    begin(2)
     begin(3)
-    flush(1)
-    flush(3)
     for k in (0, FAR):
         for c in range(2):
             exchanged(sbuf, rbuf, d_send, d_recv, k, c).wait_send()
@@ -421,9 +419,7 @@
         for c in range(CHUNKS):
             gather_part(k, c)
             for way in range(2):
-                rs(way, k + 1, c).wait_recv()
-                rs_out[way, k - 1, c] = (part[mine(way), :] + rs_in[way, k, c].astype(F32)).astype(BF)
-                rs(way, k, c).start()
+                pass_on(way, k, c)
             exchanged(sbuf, rbuf, d_send, d_recv, k, c).wait_send()
             exchanged(obuf, ybuf, r_send, r_recv, k + 1, c).wait_send()
             for way in range(2):
@@ -483,12 +479,13 @@
             pltpu.VMEM((HIDDEN, WIDTH), BF),
             pltpu.VMEM(unit, BF),
             pltpu.VMEM(unit, BF),
+            pltpu.VMEM((ROWS, HIDDEN), F32),
+            pltpu.VMEM((ROWS, HIDDEN), F32),
             pltpu.VMEM((ROWS, HIDDEN), BF),
             pltpu.VMEM(unit, BF),
             pltpu.VMEM(unit, BF),
             pltpu.VMEM((FAR + 1, 2 * TOK, ROWS), BF),
             pltpu.VMEM((2 * TOK, COLS), F32),
-            pltpu.VMEM((CHUNKS, TOK, COLS), F32),
             pltpu.VMEM((*ring, TOK, COLS), BF),
             pltpu.VMEM((*ring, TOK, COLS), BF),
             dma((CHUNKS,)), dma((3,)), dma((3,)), dma((3,)), dma, dma, dma, dma,

time: 113 us -> 111 us (0.982)
  Pallas kernels: 109 us -> 106 us
    pallas_call x1, Pallas kernels: 109 us -> 106 us  [on_device(): pl.pallas_call(kernel, out_shape=jax.ShapeDtypeStruct((TOK, WIDTH), BF),...]
where the time goes in v3:
time: 111 us; the launch traced here: 109 us
  Pallas kernels  106 us (95%)
  local copies, waits for them, and re-layouts  2.82 us (3%)
    pallas_call x1, Pallas kernels, on_device(): pl.pallas_call(kernel, out_shape=jax.ShapeDtypeStruct((TOK, WIDTH), BF),...  106 us
    unnamed x7, local copies, waits for them, and re-layouts  2.82 us

profile of v3, /device:TPU:4, one launch (start us, length us, event | category | flops | bytes accessed | tf_op | source)
XLA Modules:
  0.0 108.9 jit_solution(10407479901935125326)
XLA Ops:
  0.0 0.0 copy-start
  0.0 0.7 copy-done
  0.7 0.0 copy-start.1
  0.7 0.7 copy-done.1
  1.4 0.0 copy-start.2
  1.4 0.7 copy-done.2
  2.0 106.1 %expert_layer.1 = bf16[128,2048]{1,0:T(8,128)(2,1)S(1)} custom-call(bf16[128,2048]{1,0:T(8,128)(2,1)} %tokens.1, s32[8,128]{1,0:T(8,128)S(1)} %bitcast.2, f32[8,128]{1,0:T(8,128)S(1)} %bitcast.3, s32[1,128]{1,0:T(1,128)S(1)} %copy-done.2, bf16[1,2048,384]{2,1,0:T(8,128)(2,1)} %gate.1, bf16[1,2048,384]{2,1,0:T(8,128)(2,1)} %up.1, bf16[1,384,2048]{2,1,0:T(8,128)(2,1)} %down.1), custom_call_target="tpu_custom_call" | custom-call | tf_op jit(solution)/shard_map/expert_layer/pallas_call | solution.py:468
  108.1 0.8 copy.9
Async XLA Ops:
  0.0 0.7 copy-start
  0.7 0.7 copy-start.1
  1.4 0.7 copy-start.2

commit v4 on v3

--- a/solution.py
+++ b/solution.py
@@ -25,31 +25,39 @@
 UP, DOWN = 0, 1
 
 
+def mod(a, n):
+    return a % n if isinstance(a, int) else lax.rem(a, n)
+
+
+def div(a, n):
+    return a // n if isinstance(a, int) else lax.div(a, n)
+
+
 def kernel(
-    tokens, ids, probs, limit, gate, up, down, out,
+    tokens, route, probs, gate, up, down, out,
     tok, meta, totals, gw, uw, dw, sbuf, rbuf, gate_sum, up_sum, hid, obuf, ybuf, mix, part, rs_in, rs_out,
     in_sem, w_loc, w_send, w_recv, meta_send, meta_recv, tot_send, tot_recv,
     ag_send, ag_recv, d_send, d_recv, r_send, r_recv, rs_send, rs_recv,
 ):
     d = lax.axis_index("dp")
     c_all = lax.axis_index("expert")
-    x, z = d // NZ, d % NZ
-    y, core = c_all // 2, c_all % 2
+    x, z = div(d, NZ), mod(d, NZ)
+    y, core = div(c_all, 2), mod(c_all, 2)
     me = x * NY + y
     partner = (d, y * 2 + (1 - core))
 
     def z_peer(step):
-        return (x * NZ + (z + step) % NZ, c_all)
+        return (x * NZ + mod(z + step, NZ), c_all)
 
     def neighbour(way):
         return z_peer(1 if way == UP else NZ - 1)
 
     def xy_peer(i):
-        px, py = (x + i % NX) % NX, (y + i // NX) % NY
+        px, py = mod(x + mod(i, NX), NX), mod(y + div(i, NX), NY)
         return px * NY + py, (px * NZ + z, py * 2 + core)
 
     def x_peer(i):
-        return (((x + i) % NX) * NZ + z, c_all)
+        return (mod(x + i, NX) * NZ + z, c_all)
 
     def rows_of(chip):
         return pl.ds(pl.multiple_of(chip * UNIT, UNIT), UNIT)
@@ -61,7 +69,7 @@
         )
 
     def own_tokens(c):
-        return pltpu.make_async_copy(tokens.at[:, pl.ds(c * COLS, COLS)], tok.at[z, c], in_sem.at[c])
+        return pltpu.make_async_copy(tokens.at[:, pl.ds(c * COLS, COLS)], tok.at[z, c], in_sem)
 
     for c in range(CHUNKS):
         own_tokens(c).start()
@@ -90,14 +98,14 @@
     chosen = jnp.zeros((EXPERTS, TOK), F32)
     weight = jnp.zeros((EXPERTS, TOK), F32)
     for k in range(8):
-        hit = ids[k : k + 1, :] == row
+        hit = (route[k : k + 1, :] >> 4) == row
         chosen = jnp.where(hit, 1.0, chosen)
         weight = jnp.where(hit, probs[k : k + 1, :], weight)
     earlier = jnp.where(row < col, 1.0, 0.0).astype(BF)
     rank = jnp.dot(chosen.astype(BF), earlier, preferred_element_type=F32)
     rank = jnp.where(chosen > 0.5, rank, 1000.0).T
     weight = weight.T
-    rank = jnp.where(rank < limit[...].astype(F32), rank, 1000.0)
+    rank = jnp.where(rank < (route[0:1, :] & 15).astype(F32), rank, 1000.0)
     token_id = row.astype(F32)
     for r in range(SLOTS):
         at = rank == float(r)
@@ -109,19 +117,19 @@
         return carry
 
 
+    def unit_of(hop, c):
+        return c - 2 * div(hop, FAR) * (c // 2)
+
     def ag(way, hop, c):
-        block = (z + NZ - hop + 1) % NZ if way == UP else (z + hop - 1) % NZ
+        block = mod(z + NZ - hop + 1, NZ) if way == UP else mod(z + hop - 1, NZ)
         return remote(
-            tok.at[block, c], tok.at[block, c], ag_send.at[way, hop - 1, c], ag_recv.at[way, hop - 1, c],
+            tok.at[block, c], tok.at[block, c], ag_send, ag_recv.at[hop - 1, unit_of(hop, c)],
             neighbour(way),
         )
 
-    def ag_arrival(way, hop, c):
-        block = (z + NZ - hop) % NZ if way == UP else (z + hop) % NZ
-        return remote(
-            tok.at[block, c], tok.at[block, c], ag_send.at[way, hop - 1, c], ag_recv.at[way, hop - 1, c],
-            neighbour(way),
-        )
+    def ag_arrived(hop, c):
+        two = tok.at[pl.ds(0, 2), c]
+        remote(two, two, ag_send, ag_recv.at[hop - 1, c], z_peer(1)).wait_recv()
 
     def metas():
         several = meta.at[pl.ds(0, NZ - 1)]
@@ -147,10 +155,10 @@
         lax.fori_loop(1, NX, send_total, 0)
 
     def pair(k):
-        return (z + NZ - k) % NZ, (z + k) % NZ
+        return mod(z + NZ - k, NZ), mod(z + k, NZ)
 
     def far_chunk(k, c):
-        return c + 2 * (1 - (k % 4 + 3) // 4)
+        return c + 2 * (1 - div(mod(k, 4) + 3, 4))
 
     def slot_values(first, second):
         stacked = jnp.concatenate([first, second] * PEERS, axis=0)
@@ -170,15 +178,15 @@
 
     def exchange(src, dst, send, recv, k, c):
         def one(i, carry):
-            chip, device = xy_peer(i)
-            remote(src.at[k, c, rows_of(chip)], dst.at[k, c, rows_of(me)], send.at[k, c], recv.at[k, c], device).start()
+            chip, device = xy_peer(PEERS - i)
+            remote(src.at[k, c, rows_of(chip)], dst.at[k, c, rows_of(me)], send, recv.at[k, c], device).start()
             return carry
 
         lax.fori_loop(1, PEERS, one, 0)
 
     def exchanged(src, dst, send, recv, k, c):
         most = pl.ds(0, (PEERS - 1) * UNIT)
-        return remote(src.at[k, c, most], dst.at[k, c, most], send.at[k, c], recv.at[k, c], x_peer(1))
+        return remote(src.at[k, c, most], dst.at[k, c, most], send, recv.at[k, c], x_peer(1))
 
     def pick_rows(k, c):
         a, b = pair(k)
@@ -187,23 +195,12 @@
         rbuf[k, c, rows_of(me), :] = sbuf[k, c, rows_of(me), :]
 
     def dispatch(k, c):
-        c_b = far_chunk(k, c)
-
-        def arrive_up():
-            ag_arrival(UP, k, c).wait_recv()
-
-        def arrive_down():
-            ag_arrival(DOWN, k, c_b).wait_recv()
-
+        ag_arrived(k, c)
         if c < 2:
-            arrive_up()
             pl.when(k < FAR)(lambda: ag(UP, k + 1, c).start())
-            arrive_down()
             pl.when(k < FAR - 1)(lambda: ag(DOWN, k + 1, c).start())
         else:
-            arrive_up()
             pl.when(k < FAR - 1)(lambda: ag(UP, k + 1, c).start())
-            arrive_down()
             ag(DOWN, k + 1, c).start()
         pick_rows(k, c)
         exchange(sbuf, rbuf, d_send, d_recv, k, c)
@@ -262,15 +259,6 @@
         for i, (src, dst) in enumerate(weights):
             pltpu.make_async_copy(src, dst, w_loc.at[i]).wait()
             remote(src, theirs[i], w_send.at[i], w_recv.at[i], partner).wait_recv()
-
-    def send_back(k):
-        for c in range(2):
-            exchange(obuf, ybuf, r_send, r_recv, k, c)
-
-        @pl.when(split_k(k))
-        def _():
-            for c in range(2, CHUNKS):
-                exchange(obuf, ybuf, r_send, r_recv, k, c)
 
     def weigh_all():
         some_totals().wait_recv()
@@ -341,8 +329,7 @@
 
         return carry
 
-    for c in range(CHUNKS):
-        own_tokens(c).wait()
+    pltpu.make_async_copy(tok.at[z], tok.at[z], in_sem).wait()
     for i, (src, dst) in enumerate(weights):
         pltpu.make_async_copy(src, dst, w_loc.at[i]).start()
     mix[0] = jnp.where(selection(0), 1.0, 0.0).astype(BF)
@@ -362,14 +349,15 @@
     lax.fori_loop(1, FAR + 2, step, 0)
     for c in (0, 1):
         exchange(obuf, ybuf, r_send, r_recv, FAR, c)
-    for c in (2, 3):
-        exchange(obuf, ybuf, r_send, r_recv, FAR - 1, c)
-
     def rs(way, k, c):
+        unit = c if way == DOWN else mod(c + 2, CHUNKS)
         return remote(
-            rs_out.at[way, k - 1, c], rs_in.at[way, k - 1, c], rs_send.at[way, k - 1, c], rs_recv.at[way, k - 1, c],
-            neighbour(way),
+            rs_out.at[way, k - 1, c], rs_in.at[way, k - 1, c], rs_send, rs_recv.at[k - 1, unit], neighbour(way)
         )
+
+    def rs_arrived(k, unit):
+        two = rs_in.at[pl.ds(0, 2), k - 1, unit]
+        remote(two, two, rs_send, rs_recv.at[k - 1, unit], z_peer(1)).wait_recv()
 
     def gather_part(k, c):
         exchanged(obuf, ybuf, r_send, r_recv, k, c).wait_recv()
@@ -383,12 +371,13 @@
 
     def pass_on(way, k, c):
         chunk = chunk_of(way, c)
-        rs(way, k + 1, chunk).wait_recv()
         rs_out[way, k - 1, chunk] = (part[mine(way), :] + rs_in[way, k, chunk].astype(F32)).astype(BF)
         rs(way, k, chunk).start()
 
     def begin(c):
         gather_part(FAR - 1, c)
+        if c >= 2:
+            rs_arrived(FAR, c)
         for way in range(2):
             if c < 2:
                 rs_out[way, FAR - 2, chunk_of(way, c)] = part[mine(way), :].astype(BF)
@@ -402,29 +391,29 @@
             rs_out[way, FAR - 1, c + 2 * way] = part[way * TOK : (way + 1) * TOK, :].astype(BF)
             rs(way, FAR, c + 2 * way).start()
 
-    send_back(FAR - 2)
     begin(0)
     begin(1)
+    for c in (2, 3):
+        exchange(obuf, ybuf, r_send, r_recv, FAR - 1, c)
     begin_far(0)
+    exchange(obuf, ybuf, r_send, r_recv, FAR - 2, 0)
     begin_far(1)
-    begin(2)
-    begin(3)
-    for k in (0, FAR):
-        for c in range(2):
-            exchanged(sbuf, rbuf, d_send, d_recv, k, c).wait_send()
+    exchange(obuf, ybuf, r_send, r_recv, FAR - 2, 1)
+    for c in (2, 3):
+        begin(c)
+        exchange(obuf, ybuf, r_send, r_recv, FAR - 2, c)
 
     def collect(i, carry):
         k = FAR - 2 - i
-        send_back(k - 1)
         for c in range(CHUNKS):
             gather_part(k, c)
+            rs_arrived(k + 1, c)
             for way in range(2):
                 pass_on(way, k, c)
-            exchanged(sbuf, rbuf, d_send, d_recv, k, c).wait_send()
-            exchanged(obuf, ybuf, r_send, r_recv, k + 1, c).wait_send()
-            for way in range(2):
-                ag(way, k, c).wait_send()
-                rs(way, k + 1, c).wait_send()
+            if c < 2:
+                exchange(obuf, ybuf, r_send, r_recv, k - 1, c)
+            else:
+                pl.when(k > 1)(lambda: exchange(obuf, ybuf, r_send, r_recv, k - 1, c))
         return carry
 
     lax.fori_loop(0, FAR - 2, collect, 0)
@@ -432,35 +421,29 @@
         remote(src, dst, w_send.at[i], w_recv.at[i], partner).wait_send()
     metas().wait_send()
     some_totals().wait_send()
-    for c in range(CHUNKS):
-        exchanged(sbuf, rbuf, d_send, d_recv, FAR - 1, c).wait_send()
-        for way in range(2):
-            ag(way, FAR - 1, c).wait_send()
-        ag(c // 2, FAR, c).wait_send()
-        rs(c // 2, FAR, c).wait_send()
-    for c in range(2):
-        exchanged(obuf, ybuf, r_send, r_recv, FAR, c).wait_send()
+    blocks = tok.at[pl.ds(0, NZ - 1)]
+    remote(blocks, blocks, ag_send, ag_recv.at[0, 0], z_peer(1)).wait_send()
+    rows = sbuf.at[pl.ds(0, FAR), :, pl.ds(0, (PEERS - 1) * UNIT)]
+    remote(rows, rows, d_send, d_recv.at[0, 0], x_peer(1)).wait_send()
 
     for c in range(2):
         gather_part(0, c)
         for q in range(2):
+            rs_arrived(1, c + 2 * q)
+        for q in range(2):
             chunk = c + 2 * q
-            for way in range(2):
-                rs(way, 1, chunk).wait_recv()
             out[:, block(chunk)] = (
                 part[q * TOK : (q + 1) * TOK, :] + rs_in[UP, 0, chunk].astype(F32) + rs_in[DOWN, 0, chunk].astype(F32)
             ).astype(BF)
 
-    for c in range(CHUNKS):
-        exchanged(obuf, ybuf, r_send, r_recv, 1, c).wait_send()
-        for way in range(2):
-            rs(way, 1, c).wait_send()
-    for c in range(2):
-        exchanged(obuf, ybuf, r_send, r_recv, 0, c).wait_send()
+    remote(rows, rows, r_send, r_recv.at[0, 0], x_peer(1)).wait_send()
+    sums = rs_out.at[:, :, :, pl.ds(0, TOK * (NZ - 1) // NZ)]
+    remote(sums, sums, rs_send, rs_recv.at[0, 0], z_peer(1)).wait_send()
 
 
 def on_device(tokens, expert_ids, route_probs, shard_limit, gate_proj, up_proj, down_proj):
     dma = pltpu.SemaphoreType.DMA
+    route = expert_ids.T * 16 + shard_limit
     anywhere = pl.BlockSpec(memory_space=pltpu.HBM)
     near = pl.BlockSpec(memory_space=pltpu.VMEM)
     unit = (FAR + 1, CHUNKS, ROWS, COLS)
@@ -468,7 +451,7 @@
     return pl.pallas_call(
         kernel,
         out_shape=jax.ShapeDtypeStruct((TOK, WIDTH), BF),
-        in_specs=[anywhere, near, near, near, anywhere, anywhere, anywhere],
+        in_specs=[anywhere, near, near, anywhere, anywhere, anywhere],
         out_specs=near,
         scratch_shapes=[
             pltpu.VMEM((NZ, CHUNKS, TOK, COLS), BF),
@@ -488,16 +471,14 @@
             pltpu.VMEM((2 * TOK, COLS), F32),
             pltpu.VMEM((*ring, TOK, COLS), BF),
             pltpu.VMEM((*ring, TOK, COLS), BF),
-            dma((CHUNKS,)), dma((3,)), dma((3,)), dma((3,)), dma, dma, dma, dma,
-            dma(ring), dma(ring),
-            dma(unit[:2]), dma(unit[:2]), dma(unit[:2]), dma(unit[:2]),
-            dma(ring), dma(ring),
+            dma, dma((3,)), dma((3,)), dma((3,)), dma, dma, dma, dma,
+            dma, dma(ring[1:]), dma, dma(unit[:2]), dma, dma(unit[:2]), dma, dma(ring[1:]),
         ],
         compiler_params=pltpu.CompilerParams(
             collective_id=0, has_side_effects=True, vmem_limit_bytes=56000000
         ),
         name="expert_layer",
-    )(tokens, expert_ids.T, route_probs.T, shard_limit, gate_proj, up_proj, down_proj)
+    )(tokens, route, route_probs.T, gate_proj, up_proj, down_proj)
 
 
 def solution(mesh):

time: 111 us -> 107 us (0.964); the launches traced: 109 us -> 107 us
  Pallas kernels: 106 us -> 104 us
  local copies, waits for them, and re-layouts: 2.82 us -> 1.48 us
    pallas_call x1, Pallas kernels: 106 us -> 104 us  [on_device(): pl.pallas_call(kernel, out_shape=jax.ShapeDtypeStruct((TOK, WIDTH), BF),...]
    unnamed x7 -> x3, local copies, waits for them, and re-layouts: 2.82 us -> 1.48 us
where the time goes in v4:
time: 107 us
  Pallas kernels  104 us (97%)
  local copies, waits for them, and re-layouts  1.48 us (1%)
    pallas_call x1, Pallas kernels, on_device(): pl.pallas_call(kernel, out_shape=jax.ShapeDtypeStruct((TOK, WIDTH), BF),...  104 us

profile of v4, /device:TPU:4, one launch (start us, length us, event | category | flops | bytes accessed | tf_op | source)
XLA Modules:
  0.0 106.6 jit_solution(15995247491270428645)
XLA Ops:
  0.0 0.7 add_bitcast_fusion.route
  0.7 0.0 copy-start
  0.7 0.7 copy-done
  1.4 104.4 %expert_layer.1 = bf16[128,2048]{1,0:T(8,128)(2,1)S(1)} custom-call(bf16[128,2048]{1,0:T(8,128)(2,1)} %tokens.1, s32[8,128]{1,0:T(8,128)S(1)} %add_bitcast_fusion.route, f32[8,128]{1,0:T(8,128)S(1)} %bitcast.4, bf16[1,2048,384]{2,1,0:T(8,128)(2,1)} %gate.1, bf16[1,2048,384]{2,1,0:T(8,128)(2,1)} %up.1, bf16[1,384,2048]{2,1,0:T(8,128)(2,1)} %down.1), custom_call_target="tpu_custom_call" | custom-call | tf_op jit(solution)/shard_map/expert_layer/pallas_call | solution.py:451
  105.8 0.8 copy.9
Async XLA Ops:
  0.7 0.7 copy-start

commit v5 on v4

--- a/solution.py
+++ b/solution.py
@@ -34,9 +34,9 @@
 
 
 def kernel(
-    tokens, route, probs, gate, up, down, out,
-    tok, meta, totals, gw, uw, dw, sbuf, rbuf, gate_sum, up_sum, hid, obuf, ybuf, mix, part, rs_in, rs_out,
-    in_sem, w_loc, w_send, w_recv, meta_send, meta_recv, tot_send, tot_recv,
+    tokens, ids_in, probs_in, limit_in, gate, up, down, out,
+    ids, probs, limit, tok, meta, totals, gw, uw, dw, sbuf, rbuf, gate_sum, up_sum, hid, obuf, ybuf, mix, part, rs_in, rs_out,
+    route_sem, in_sem, w_loc, w_send, w_recv, meta_send, meta_recv, tot_send, tot_recv,
     ag_send, ag_recv, d_send, d_recv, r_send, r_recv, rs_send, rs_recv,
 ):
     d = lax.axis_index("dp")
@@ -71,6 +71,9 @@
     def own_tokens(c):
         return pltpu.make_async_copy(tokens.at[:, pl.ds(c * COLS, COLS)], tok.at[z, c], in_sem)
 
+    routing = ((ids_in, ids), (probs_in, probs), (limit_in, limit))
+    for i, (src, dst) in enumerate(routing):
+        pltpu.make_async_copy(src, dst, route_sem.at[i]).start()
     for c in range(CHUNKS):
         own_tokens(c).start()
     wide = pl.ds(pl.multiple_of(core * (HIDDEN // 2), HIDDEN // 2), HIDDEN // 2)
@@ -95,17 +98,19 @@
 
     col = lax.broadcasted_iota(jnp.int32, (EXPERTS, TOK), 1)
     row = lax.broadcasted_iota(jnp.int32, (EXPERTS, TOK), 0)
+    for i, (src, dst) in enumerate(routing):
+        pltpu.make_async_copy(src, dst, route_sem.at[i]).wait()
     chosen = jnp.zeros((EXPERTS, TOK), F32)
     weight = jnp.zeros((EXPERTS, TOK), F32)
     for k in range(8):
-        hit = (route[k : k + 1, :] >> 4) == row
+        hit = ids[k : k + 1, :] == row
         chosen = jnp.where(hit, 1.0, chosen)
         weight = jnp.where(hit, probs[k : k + 1, :], weight)
     earlier = jnp.where(row < col, 1.0, 0.0).astype(BF)
     rank = jnp.dot(chosen.astype(BF), earlier, preferred_element_type=F32)
     rank = jnp.where(chosen > 0.5, rank, 1000.0).T
     weight = weight.T
-    rank = jnp.where(rank < (route[0:1, :] & 15).astype(F32), rank, 1000.0)
+    rank = jnp.where(rank < limit[...].astype(F32), rank, 1000.0)
     token_id = row.astype(F32)
     for r in range(SLOTS):
         at = rank == float(r)
@@ -180,6 +185,20 @@
         def one(i, carry):
             chip, device = xy_peer(PEERS - i)
             remote(src.at[k, c, rows_of(chip)], dst.at[k, c, rows_of(me)], send, recv.at[k, c], device).start()
+            return carry
+
+        lax.fori_loop(1, PEERS, one, 0)
+
+    def half_of(h):
+        return pl.ds(h * (COLS // 2), COLS // 2)
+
+    def exchange_half(h):
+        def one(i, carry):
+            chip, device = xy_peer(PEERS - i)
+            remote(
+                obuf.at[FAR - 1, 0, rows_of(chip), half_of(h)], ybuf.at[FAR - 1, 0, rows_of(me), half_of(h)],
+                r_send, r_recv.at[0, 2 + h], device,
+            ).start()
             return carry
 
         lax.fori_loop(1, PEERS, one, 0)
@@ -322,8 +341,9 @@
 
                 @pl.when(k == FAR)
                 def _():
-                    for early in range(2):
-                        exchange(obuf, ybuf, r_send, r_recv, FAR - 1, early)
+                    for h in range(2):
+                        exchange_half(h)
+                    exchange(obuf, ybuf, r_send, r_recv, FAR - 1, 1)
                     weigh_all()
                     add_chunk(FAR, 0, True, True)
 
@@ -391,7 +411,18 @@
             rs_out[way, FAR - 1, c + 2 * way] = part[way * TOK : (way + 1) * TOK, :].astype(BF)
             rs(way, FAR, c + 2 * way).start()
 
-    begin(0)
+    for h in range(2):
+        most = ybuf.at[FAR - 1, 0, pl.ds(0, (PEERS - 1) * UNIT), half_of(h)]
+        remote(most, most, r_send, r_recv.at[0, 2 + h], x_peer(1)).wait_recv()
+        cols = slice(h * (COLS // 2), (h + 1) * (COLS // 2))
+        value = jnp.dot(mix[FAR - 1], ybuf[FAR - 1, 0, :, cols], preferred_element_type=F32)
+        for way in range(2):
+            chunk = chunk_of(way, 0)
+            rs_out[way, FAR - 2, chunk, :, cols] = value[mine(way), :].astype(BF)
+            remote(
+                rs_out.at[way, FAR - 2, chunk, :, half_of(h)], rs_in.at[way, FAR - 2, chunk, :, half_of(h)],
+                rs_send, rs_recv.at[FAR - 2, 0], neighbour(way),
+            ).start()
     begin(1)
     for c in (2, 3):
         exchange(obuf, ybuf, r_send, r_recv, FAR - 1, c)
@@ -443,17 +474,20 @@
 
 def on_device(tokens, expert_ids, route_probs, shard_limit, gate_proj, up_proj, down_proj):
     dma = pltpu.SemaphoreType.DMA
-    route = expert_ids.T * 16 + shard_limit
     anywhere = pl.BlockSpec(memory_space=pltpu.HBM)
     near = pl.BlockSpec(memory_space=pltpu.VMEM)
     unit = (FAR + 1, CHUNKS, ROWS, COLS)
+    operands = (tokens, expert_ids.T, route_probs.T, shard_limit, gate_proj, up_proj, down_proj)
     ring = (2, FAR, CHUNKS)
     return pl.pallas_call(
         kernel,
         out_shape=jax.ShapeDtypeStruct((TOK, WIDTH), BF),
-        in_specs=[anywhere, near, near, anywhere, anywhere, anywhere],
+        in_specs=[anywhere] * len(operands),
         out_specs=near,
         scratch_shapes=[
+            pltpu.VMEM((8, TOK), jnp.int32),
+            pltpu.VMEM((8, TOK), F32),
+            pltpu.VMEM((1, EXPERTS), jnp.int32),
             pltpu.VMEM((NZ, CHUNKS, TOK, COLS), BF),
             pltpu.VMEM((NZ, 2 * SLOTS, EXPERTS), F32),
             pltpu.VMEM((NX, 8, EXPERTS), F32),
@@ -471,14 +505,14 @@
             pltpu.VMEM((2 * TOK, COLS), F32),
             pltpu.VMEM((*ring, TOK, COLS), BF),
             pltpu.VMEM((*ring, TOK, COLS), BF),
-            dma, dma((3,)), dma((3,)), dma((3,)), dma, dma, dma, dma,
+            dma((3,)), dma, dma((3,)), dma((3,)), dma((3,)), dma, dma, dma, dma,
             dma, dma(ring[1:]), dma, dma(unit[:2]), dma, dma(unit[:2]), dma, dma(ring[1:]),
         ],
         compiler_params=pltpu.CompilerParams(
             collective_id=0, has_side_effects=True, vmem_limit_bytes=56000000
         ),
         name="expert_layer",
-    )(tokens, route, route_probs.T, gate_proj, up_proj, down_proj)
+    )(*(pltpu.with_memory_space_constraint(array, pltpu.HBM) for array in operands))
 
 
 def solution(mesh):

time: 107 us -> 107 us (level); the launches traced: 107 us -> 105 us
  no operation moved by 1% of the time
where the time goes in v5:
time: 107 us; the launch traced here: 105 us
  Pallas kernels  104 us (97%)
    pallas_call x1, Pallas kernels, on_device(): pl.pallas_call(kernel, out_shape=jax.ShapeDtypeStruct((TOK, WIDTH), BF),...  104 us

profile of v5, /device:TPU:4, one launch (start us, length us, event | category | flops | bytes accessed | tf_op | source)
XLA Modules:
  0.0 104.7 jit_solution(4723661435129442701)
XLA Ops:
  0.0 103.9 %expert_layer.1 = bf16[128,2048]{1,0:T(8,128)(2,1)S(1)} custom-call(bf16[128,2048]{1,0:T(8,128)(2,1)} %tokens.1, s32[8,128]{1,0:T(8,128)} %bitcast.2, f32[8,128]{1,0:T(8,128)} %bitcast.3, s32[1,128]{1,0:T(1,128)} %limit_in.1, bf16[1,2048,384]{2,1,0:T(8,128)(2,1)} %gate.1, bf16[1,2048,384]{2,1,0:T(8,128)(2,1)} %up.1, bf16[1,384,2048]{2,1,0:T(8,128)(2,1)} %down.1), custom_call_target="tpu_custom_call" | custom-call | tf_op jit(solution)/shard_map/expert_layer/pallas_call | solution.py:482
  103.9 0.8 copy.9

commit v6 on v5

--- a/solution.py
+++ b/solution.py
@@ -35,7 +35,7 @@
 
 def kernel(
     tokens, ids_in, probs_in, limit_in, gate, up, down, out,
-    ids, probs, limit, tok, meta, totals, gw, uw, dw, sbuf, rbuf, gate_sum, up_sum, hid, obuf, ybuf, mix, part, rs_in, rs_out,
+    ids, probs, limit, tok, meta, totals, gw, uw, dw, sbuf, rbuf, gate_sum, up_sum, hid, obuf, ybuf, mix, back, part, rs_in, rs_out,
     route_sem, in_sem, w_loc, w_send, w_recv, meta_send, meta_recv, tot_send, tot_recv,
     ag_send, ag_recv, d_send, d_recv, r_send, r_recv, rs_send, rs_recv,
 ):
@@ -279,8 +279,7 @@
             pltpu.make_async_copy(src, dst, w_loc.at[i]).wait()
             remote(src, theirs[i], w_send.at[i], w_recv.at[i], partner).wait_recv()
 
-    def weigh_all():
-        some_totals().wait_recv()
+    def weigh(first, last):
         before_x = jnp.zeros((1, EXPERTS), F32)
         for s in range(NX):
             before_x = before_x + jnp.where(s < x, 1.0, 0.0) * totals[s, 0:1, :]
@@ -292,13 +291,13 @@
             r = lax.broadcasted_iota(jnp.int32, (SLOTS, EXPERTS), 0).astype(F32)
             return jnp.where(offset + r < float(COL_CAP), meta[shard, SLOTS : 2 * SLOTS, :], 0.0)
 
-        def weigh(k, carry):
+        def one(k, carry):
             a, b = pair(k)
             w = slot_values(kept_weight(a), kept_weight(b))
-            mix[k] = jnp.where(selection(k), w, 0.0).T.astype(BF)
+            back[k] = jnp.where(selection(k), w, 0.0).T.astype(BF)
             return carry
 
-        lax.fori_loop(0, FAR + 1, weigh, 0)
+        lax.fori_loop(first, last, one, 0)
 
     def step(k, carry):
         @pl.when(k == 1)
@@ -317,6 +316,10 @@
                 pl.when(split_k(k))(lambda: dispatch(k, c))
             if c < 2:
                 pl.when((k > 1) & (k <= FAR))(lambda: add_chunk(k - 1, c + 1, False, False))
+            if c == 1:
+                pl.when(k == 2)(lambda: some_totals().wait_recv())
+                pl.when((k > 1) & (k < FAR))(lambda: weigh(2 * k - 4, 2 * k - 2))
+                pl.when(k == FAR)(lambda: weigh(FAR, FAR + 1))
             if c == 2:
                 @pl.when(k == 1)
                 def _():
@@ -344,7 +347,6 @@
                     for h in range(2):
                         exchange_half(h)
                     exchange(obuf, ybuf, r_send, r_recv, FAR - 1, 1)
-                    weigh_all()
                     add_chunk(FAR, 0, True, True)
 
         return carry
@@ -367,8 +369,6 @@
         remote(src, dst, w_send.at[i], w_recv.at[i], partner).start()
 
     lax.fori_loop(1, FAR + 2, step, 0)
-    for c in (0, 1):
-        exchange(obuf, ybuf, r_send, r_recv, FAR, c)
     def rs(way, k, c):
         unit = c if way == DOWN else mod(c + 2, CHUNKS)
         return remote(
@@ -381,7 +381,7 @@
 
     def gather_part(k, c):
         exchanged(obuf, ybuf, r_send, r_recv, k, c).wait_recv()
-        part[...] = jnp.dot(mix[k], ybuf[k, c], preferred_element_type=F32)
+        part[...] = jnp.dot(back[k], ybuf[k, c], preferred_element_type=F32)
 
     def mine(way):
         return slice(TOK, 2 * TOK) if way == UP else slice(0, TOK)
@@ -415,7 +415,7 @@
         most = ybuf.at[FAR - 1, 0, pl.ds(0, (PEERS - 1) * UNIT), half_of(h)]
         remote(most, most, r_send, r_recv.at[0, 2 + h], x_peer(1)).wait_recv()
         cols = slice(h * (COLS // 2), (h + 1) * (COLS // 2))
-        value = jnp.dot(mix[FAR - 1], ybuf[FAR - 1, 0, :, cols], preferred_element_type=F32)
+        value = jnp.dot(back[FAR - 1], ybuf[FAR - 1, 0, :, cols], preferred_element_type=F32)
         for way in range(2):
             chunk = chunk_of(way, 0)
             rs_out[way, FAR - 2, chunk, :, cols] = value[mine(way), :].astype(BF)
@@ -423,6 +423,7 @@
                 rs_out.at[way, FAR - 2, chunk, :, half_of(h)], rs_in.at[way, FAR - 2, chunk, :, half_of(h)],
                 rs_send, rs_recv.at[FAR - 2, 0], neighbour(way),
             ).start()
+        exchange(obuf, ybuf, r_send, r_recv, FAR, h)
     begin(1)
     for c in (2, 3):
         exchange(obuf, ybuf, r_send, r_recv, FAR - 1, c)
@@ -502,6 +503,7 @@
             pltpu.VMEM(unit, BF),
             pltpu.VMEM(unit, BF),
             pltpu.VMEM((FAR + 1, 2 * TOK, ROWS), BF),
+            pltpu.VMEM((FAR + 1, 2 * TOK, ROWS), BF),
             pltpu.VMEM((2 * TOK, COLS), F32),
             pltpu.VMEM((*ring, TOK, COLS), BF),
             pltpu.VMEM((*ring, TOK, COLS), BF),

time: 107 us -> 106 us (level); the launches traced: 105 us -> 105 us
  no operation moved by 1% of the time
where the time goes in v6:
time: 106 us; the launch traced here: 105 us
  Pallas kernels  104 us (98%)
    pallas_call x1, Pallas kernels, on_device(): pl.pallas_call(kernel, out_shape=jax.ShapeDtypeStruct((TOK, WIDTH), BF),...  104 us

profile of v6, /device:TPU:4, one launch (start us, length us, event | category | flops | bytes accessed | tf_op | source)
XLA Modules:
  0.0 105.0 jit_solution(16598988646441196344)
XLA Ops:
  0.0 104.2 %expert_layer.1 = bf16[128,2048]{1,0:T(8,128)(2,1)S(1)} custom-call(bf16[128,2048]{1,0:T(8,128)(2,1)} %tokens.1, s32[8,128]{1,0:T(8,128)} %bitcast.2, f32[8,128]{1,0:T(8,128)} %bitcast.3, s32[1,128]{1,0:T(1,128)} %limit_in.1, bf16[1,2048,384]{2,1,0:T(8,128)(2,1)} %gate.1, bf16[1,2048,384]{2,1,0:T(8,128)(2,1)} %up.1, bf16[1,384,2048]{2,1,0:T(8,128)(2,1)} %down.1), custom_call_target="tpu_custom_call" | custom-call | tf_op jit(solution)/shard_map/expert_layer/pallas_call | solution.py:483
  104.2 0.8 copy.9

commit v7 on v6

--- a/solution.py
+++ b/solution.py
@@ -117,10 +117,9 @@
         meta[z, r : r + 1, :] = jnp.sum(jnp.where(at, token_id + 1000.0, 0.0), axis=0, keepdims=True) - 1000.0
         meta[z, SLOTS + r : SLOTS + r + 1, :] = jnp.sum(jnp.where(at, weight, 0.0), axis=0, keepdims=True)
 
-    def send_meta(i, carry):
-        remote(meta.at[z], meta.at[z], meta_send, meta_recv, z_peer(i)).start()
-        return carry
-
+    def send_metas():
+        for i in (1, 7, 2, 6, 3, 5, 4):
+            remote(meta.at[z], meta.at[z], meta_send, meta_recv.at[min(i, NZ - i) - 1], z_peer(i)).start()
 
     def unit_of(hop, c):
         return c - 2 * div(hop, FAR) * (c // 2)
@@ -136,9 +135,9 @@
         two = tok.at[pl.ds(0, 2), c]
         remote(two, two, ag_send, ag_recv.at[hop - 1, c], z_peer(1)).wait_recv()
 
-    def metas():
-        several = meta.at[pl.ds(0, NZ - 1)]
-        return remote(several, several, meta_send, meta_recv, z_peer(1))
+    def metas(k, number):
+        several = meta.at[pl.ds(0, number)]
+        return remote(several, several, meta_send, meta_recv.at[k - 1], z_peer(1))
 
     def some_totals():
         some = totals.at[pl.ds(0, NX - 1)]
@@ -302,7 +301,13 @@
     def step(k, carry):
         @pl.when(k == 1)
         def _():
-            metas().wait_recv()
+            metas(1, 2).wait_recv()
+
+        @pl.when(k == 2)
+        def _():
+            metas(2, 2).wait_recv()
+            metas(3, 2).wait_recv()
+            metas(FAR, 1).wait_recv()
             send_totals()
 
         @pl.when(k <= FAR)
@@ -317,9 +322,9 @@
             if c < 2:
                 pl.when((k > 1) & (k <= FAR))(lambda: add_chunk(k - 1, c + 1, False, False))
             if c == 1:
-                pl.when(k == 2)(lambda: some_totals().wait_recv())
-                pl.when((k > 1) & (k < FAR))(lambda: weigh(2 * k - 4, 2 * k - 2))
-                pl.when(k == FAR)(lambda: weigh(FAR, FAR + 1))
+                pl.when(k == FAR - 1)(lambda: some_totals().wait_recv())
+                pl.when(k == FAR - 1)(lambda: weigh(0, 3))
+                pl.when(k == FAR)(lambda: weigh(3, FAR + 1))
             if c == 2:
                 @pl.when(k == 1)
                 def _():
@@ -359,7 +364,7 @@
         pick_rows(0, c)
 
     pl.semaphore_wait(barrier, NZ - 1 + PEERS - 1 + 1)
-    lax.fori_loop(1, NZ, send_meta, 0)
+    send_metas()
     for c in range(CHUNKS):
         for way in range(2):
             ag(way, 1, c).start()
@@ -451,7 +456,7 @@
     lax.fori_loop(0, FAR - 2, collect, 0)
     for i, (src, dst) in enumerate(weights):
         remote(src, dst, w_send.at[i], w_recv.at[i], partner).wait_send()
-    metas().wait_send()
+    metas(1, NZ - 1).wait_send()
     some_totals().wait_send()
     blocks = tok.at[pl.ds(0, NZ - 1)]
     remote(blocks, blocks, ag_send, ag_recv.at[0, 0], z_peer(1)).wait_send()
@@ -507,7 +512,7 @@
             pltpu.VMEM((2 * TOK, COLS), F32),
             pltpu.VMEM((*ring, TOK, COLS), BF),
             pltpu.VMEM((*ring, TOK, COLS), BF),
-            dma((3,)), dma, dma((3,)), dma((3,)), dma((3,)), dma, dma, dma, dma,
+            dma((3,)), dma, dma((3,)), dma((3,)), dma((3,)), dma, dma((FAR,)), dma, dma,
             dma, dma(ring[1:]), dma, dma(unit[:2]), dma, dma(unit[:2]), dma, dma(ring[1:]),
         ],
         compiler_params=pltpu.CompilerParams(

time: 106 us -> 106 us (level)
  no operation moved by 1% of the time
where the time goes in v7:
time: 106 us; the launch traced here: 105 us
  Pallas kernels  104 us (98%)
    pallas_call x1, Pallas kernels, on_device(): pl.pallas_call(kernel, out_shape=jax.ShapeDtypeStruct((TOK, WIDTH), BF),...  104 us

profile of v7, /device:TPU:4, one launch (start us, length us, event | category | flops | bytes accessed | tf_op | source)
XLA Modules:
  0.0 104.9 jit_solution(13083348995413534204)
XLA Ops:
  0.0 104.1 %expert_layer.1 = bf16[128,2048]{1,0:T(8,128)(2,1)S(1)} custom-call(bf16[128,2048]{1,0:T(8,128)(2,1)} %tokens.1, s32[8,128]{1,0:T(8,128)} %bitcast.2, f32[8,128]{1,0:T(8,128)} %bitcast.3, s32[1,128]{1,0:T(1,128)} %limit_in.1, bf16[1,2048,384]{2,1,0:T(8,128)(2,1)} %gate.1, bf16[1,2048,384]{2,1,0:T(8,128)(2,1)} %up.1, bf16[1,384,2048]{2,1,0:T(8,128)(2,1)} %down.1), custom_call_target="tpu_custom_call" | custom-call | tf_op jit(solution)/shard_map/expert_layer/pallas_call | solution.py:488
  104.1 0.8 copy.9
